TPU v7x, 256 devices: a whole 4x4x8 slice. The times are simulated.
256 devices in a mesh: gx: 16 (over y_hi, z), gy: 16 (over x, y_lo, core).
Axes of the slice: x: 4, y: 4 (y_hi: 2, y_lo: 2; y = y_hi * 2 + y_lo), z: 8, core: 2. Of those that a mesh axis runs over, the one named last changes fastest.
Arguments:
- tokens: bfloat16 [256, 8192], P('gy', 'gx'), may hold values from -6 to 6
- target: bfloat16 [256, 8192], P('gy', 'gx'), may hold values from -6 to 6
- w_gate: bfloat16 [8192, 14336], P('gx', 'gy'), may hold values from -0.0625 to 0.0625
- w_up: bfloat16 [8192, 14336], P('gx', 'gy'), may hold values from -0.0625 to 0.0625
- w_down: bfloat16 [14336, 8192], P('gy', 'gx'), may hold values from -0.046875 to 0.046875
- t_gate: bfloat16 [8192, 14336], P('gx', 'gy'), may hold values from -0.0625 to 0.0625
- t_up: bfloat16 [8192, 14336], P('gx', 'gy'), may hold values from -0.0625 to 0.0625
- t_down: bfloat16 [14336, 8192], P('gy', 'gx'), may hold values from -0.046875 to 0.046875
Outputs:
- hvp_gate: bfloat16 [8192, 14336], P('gx', 'gy')
- hvp_up: bfloat16 [8192, 14336], P('gx', 'gy')
- hvp_down: bfloat16 [14336, 8192], P('gy', 'gx')
All inputs are finite; a program needn't handle non-finite values.
Results may differ from a plain program's by a relative error of at most 0.0074.
Values may be sent and summed in bfloat16 or wider, within the bound.
A program may use at most 64 MiB of HBM per device.

v0:
```python
import math

import jax
import jax.numpy as jnp
from jax import lax
from jax.sharding import Mesh
from jax.sharding import PartitionSpec as P

TOKENS = 256
GX = ("gx_0", "gx_1")


def copy_for_each(value, axis):
    copies = jnp.broadcast_to(value, (lax.axis_size(axis), *value.shape))
    return lax.all_to_all(copies, axis, split_axis=0, concat_axis=0, tiled=True)


def joined_along(parts, dim):
    lengths = list(parts.shape[1:])
    lengths[dim] *= parts.shape[0]
    return jnp.moveaxis(parts, 0, dim).reshape(lengths)


def gathered_copies(value, axis, dim):
    parts = copy_for_each(value, axis)
    return joined_along(parts, dim)


def reduced_to_own(parts, axes, turns):
    lengths = [lax.axis_size(a) for a in axes]
    parts = parts.reshape(*lengths, *parts.shape[1:])
    parts = parts.transpose(*turns, *range(len(axes), parts.ndim))
    parts = parts.reshape(-1, *parts.shape[len(axes) :])
    for k in turns:
        parts = lax.psum_scatter(parts, axes[k], scatter_dimension=0, tiled=True)
    return parts[0]


def split_up(value, dim, length):
    lengths = value.shape
    parts = value.reshape(*lengths[:dim], length, lengths[dim] // length, *lengths[dim + 1 :])
    return jnp.moveaxis(parts, dim, 0)


def sum_by_axis(value, axes, turns, dim):
    length = lax.axis_size(axes)
    return reduced_to_own(split_up(value, dim, length), axes, turns)


def sent_together(arrays, axis, dim, along):
    both = jnp.concatenate(arrays, axis=along)
    filled, at, outs = (lax.all_gather(both, axis, axis=dim, tiled=True), 0, [])
    for a in arrays:
        outs.append(lax.slice_in_dim(filled, at, at + a.shape[along], axis=along))
        at += a.shape[along]
    return tuple(outs)


def sum_at_owner(value, axis, dim):
    length = lax.axis_size(axis)
    parts = lax.all_to_all(split_up(value, dim, length), axis, 0, 0, tiled=True)
    return jnp.sum(parts, axis=0)


def summed_on_arrival(value, axis, dim):
    parts = split_up(value, dim, lax.axis_size(axis))
    arrived = lax.all_to_all(parts, axis, split_axis=0, concat_axis=0, tiled=True)
    return arrived.astype(jnp.float32).sum(axis=0)


def silu_parts(gate):
    sig = jax.nn.sigmoid(gate)
    first = sig * (1.0 + gate * (1.0 - sig))
    second = sig * (1.0 - sig) * (2.0 + gate * (1.0 - 2.0 * sig))
    return (gate * sig, first, second)


def matmul(left, right):
    return jnp.dot(left, right, preferred_element_type=jnp.float32)


def lead_dot(left, right):
    return lax.dot_general(
        left, right, (((0,), (0,)), ((), ())), preferred_element_type=jnp.float32
    )


def tail_dot(left, right):
    return lax.dot_general(
        left, right, (((1,), (1,)), ((), ())), preferred_element_type=jnp.float32
    )


def body(tokens, target, w_gate, w_up, w_down, t_gate, t_up, t_down):
    scale = 1.0 / math.sqrt(TOKENS)
    width = w_gate.shape[1]
    dlocal = w_down.shape[1]
    xfull = gathered_copies(tokens, "gy", 0)
    w_joined = jnp.concatenate([w_gate, w_up, t_gate, t_up], 1)
    rows = xfull
    summed = sum_by_axis(matmul(rows, w_joined), GX, (1, 0), 0)
    gate = summed[:, :width]
    upper = summed[:, width : 2 * width]
    gate_dot = summed[:, 2 * width : 3 * width]
    upper_dot = summed[:, 3 * width :]
    silu_val, first, second = silu_parts(gate)
    hidden = (silu_val * upper).astype(jnp.bfloat16)
    hidden_dot = (first * gate_dot * upper + silu_val * upper_dot).astype(jnp.bfloat16)
    hid_full, hid_dot_full = sent_together((hidden, hidden_dot), GX, 0, 1)
    rows = hid_full
    rows_dot = hid_dot_full
    output = matmul(rows, w_down)
    output_dot = matmul(rows_dot, w_down) + matmul(rows, t_down)
    outputs = sum_at_owner(jnp.concatenate([output, output_dot], 1), "gy", 0)
    grad = ((outputs[:, :dlocal] - target.astype(jnp.float32)) * scale).astype(jnp.bfloat16)
    grad_dot = (outputs[:, dlocal:] * scale).astype(jnp.bfloat16)
    grad_full, grad_dot_full = sent_together((grad, grad_dot), "gy", 0, 1)
    hvp_down = (lead_dot(hid_dot_full, grad_full) + lead_dot(hid_full, grad_dot_full)).astype(
        jnp.bfloat16
    )
    rows = grad_full
    rows_dot = grad_dot_full
    back = tail_dot(rows, w_down)
    back_dot = tail_dot(rows_dot, w_down) + tail_dot(rows, t_down)
    backs = summed_on_arrival(jnp.concatenate([back, back_dot], 1).astype(jnp.bfloat16), GX, 0)
    back = backs[:, :width]
    back_dot = backs[:, width:]
    gate_in = (
        back_dot * upper * first + back * upper_dot * first + back * upper * second * gate_dot
    ).astype(jnp.bfloat16)
    upper_in = (back_dot * silu_val + back * first * gate_dot).astype(jnp.bfloat16)
    gate_full, upper_full = sent_together((gate_in, upper_in), GX, 0, 1)
    hvp_gate = lead_dot(xfull, gate_full).astype(jnp.bfloat16)
    hvp_up = lead_dot(xfull, upper_full).astype(jnp.bfloat16)
    return (hvp_gate, hvp_up, hvp_down)


def solution(mesh):
    finer = Mesh(mesh.devices.reshape(2, 8, mesh.shape["gy"]), ("gx_0", "gx_1", "gy"))
    in_specs = (
        P("gy", GX),
        P("gy", GX),
        P(GX, "gy"),
        P(GX, "gy"),
        P("gy", GX),
        P(GX, "gy"),
        P(GX, "gy"),
        P("gy", GX),
    )
    out_specs = (P(GX, "gy"), P(GX, "gy"), P("gy", GX))
    return jax.shard_map(body, mesh=finer, in_specs=in_specs, out_specs=out_specs, check_vma=False)
```

profile of v0, /device:TPU:32, one launch (start us, length us, event | category | flops | bytes accessed | tf_op | source)
XLA Modules:
  0.0 271.2 jit_solution(16480847980377072094)
XLA Ops:
  7.2 0.0 reduce-scatter.3.cloned.1.call-start
  7.2 0.8 broadcast_in_dim.3
  8.0 12.9 %all_to_all.15 = bf16[16,16,512]{2,1,0:T(8,128)(2,1)S(1)} all-to-all(bf16[16,16,512]{2,1,0:T(8,128)(2,1)S(1)} %broadcast_in_dim.3), channel_id=1, replica_groups=mesh['gx_0'=2,'gx_1'=8,'gy'=16] {'gy'}, dimensions={0} | all-to-all | bytes 524288 | tf_op jit(solution)/shard_map/all_to_all | solution.py:15
  20.9 3.1 %fusion = f32[3584,256]{0,1:T(8,128)S(1)} fusion(bf16[256,512]{1,0:T(8,128)(2,1)S(1)} %bitcast.27, bf16[512,896]{1,0:T(8,128)(2,1)} %param.14, bf16[512,896]{1,0:T(8,128)(2,1)} %param.13, bf16[512,896]{1,0:T(8,128)(2,1)} %param.11, bf16[512,896]{1,0:T(8,128)(2,1)} %param.10), kind=kOutput, calls=%fused_computation | convolution fusion | flops 954204160 | bytes 7602176 | tf_op jit(solution)/shard_map/dot_general | solution.py:79
  24.1 2.1 copy.13
  26.2 0.0 reduce-scatter.5.cloned.1.call-start
  26.2 49.6 %reduce-scatter.3.cloned.1.call-done = f32[2,16,3584]{2,1,0:T(8,128)} async-done(((f32[16,16,3584]{2,1,0:T(8,128)}), f32[2,16,3584]{2,1,0:T(8,128)}) %reduce-scatter.3.cloned.1.call-update) | async-done | bytes 458768 | tf_op jit(solution)/shard_map/reduce_scatter | solution.py:35
  75.8 23.6 %reduce-scatter.5.cloned.1.call-done = f32[1,16,3584]{2,1,0:T(8,128)} async-done(((f32[2,16,3584]{2,1,0:T(8,128)}), f32[1,16,3584]{2,1,0:T(8,128)}) %reduce-scatter.5.cloned.1.call-update) | async-done | bytes 229392 | tf_op jit(solution)/shard_map/reduce_scatter | solution.py:35
  99.4 1.0 multiply_convert_fusion
  100.4 41.3 %all_gather.9 = bf16[256,1792]{1,0:T(8,128)(2,1)S(1)} all-gather(bf16[16,1792]{1,0:T(8,128)(2,1)S(1)} %pad_maximum_fusion.2), channel_id=1, replica_groups=mesh['gx_0'=2,'gx_1'=8,'gy'=16] {'gx_0','gx_1'}, dimensions={0}, use_global_device_ids=true | all-gather | bytes 974848 | tf_op jit(solution)/shard_map/all_gather | solution.py:52
  141.7 0.4 fusion.15
  142.1 0.4 fusion.19
  142.6 0.4 convolution_add_fusion.1
  143.0 0.1 pad_maximum_fusion
  143.1 20.6 %all_to_all.16 = f32[16,16,1024]{2,1,0:T(8,128)S(1)} all-to-all(f32[16,16,1024]{2,1,0:T(8,128)S(1)} %bitcast.25), channel_id=1, replica_groups=mesh['gx_0'=2,'gx_1'=8,'gy'=16] {'gy'}, dimensions={0} | all-to-all | bytes 2097152 | tf_op jit(solution)/shard_map/all_to_all | solution.py:61
  163.8 0.1 reduce_sum.18
  163.9 18.1 %all_gather.10 = bf16[256,1024]{1,0:T(8,128)(2,1)S(1)} all-gather(bf16[16,1024]{1,0:T(8,128)(2,1)S(1)} %pad_maximum_fusion.4), channel_id=1, replica_groups=mesh['gx_0'=2,'gx_1'=8,'gy'=16] {'gy'}, dimensions={0}, use_global_device_ids=true | all-gather | bytes 557056 | tf_op jit(solution)/shard_map/all_gather | solution.py:52
  181.9 0.5 convolution_convert_fusion.2
  182.4 0.5 fusion.22
  182.9 0.5 fusion.10
  183.4 1.0 pad_maximum_fusion.1
  184.4 8.1 %all-to-all-start.2 = ((bf16[16,16,1792]{2,1,0:T(8,128)(2,1)}), bf16[16,16,1792]{2,1,0:T(8,128)(2,1)S(1)}, u32[]{:S(2)}, u32[]{:S(2)}) async-start(bf16[16,16,1792]{2,1,0:T(8,128)(2,1)} %pad_maximum_fusion.1), calls=%async_computation.4 | async-start | bytes 1835008 | tf_op jit(solution)/shard_map/all_to_all | solution.py:67
  192.5 0.4 fusion.13
  192.9 1.4 add_convert_fusion
  194.3 23.5 %all-to-all-done.2 = bf16[16,16,1792]{2,1,0:T(8,128)(2,1)S(1)} async-done(((bf16[16,16,1792]{2,1,0:T(8,128)(2,1)}), bf16[16,16,1792]{2,1,0:T(8,128)(2,1)S(1)}, u32[]{:S(2)}, u32[]{:S(2)}) %all-to-all-start.2) | async-done | bytes 917536 | tf_op jit(solution)/shard_map/all_to_all | solution.py:67
  217.8 0.1 convert_reduce_fusion
  217.9 1.0 fusion.33
  218.9 42.0 %all_gather.11 = bf16[256,1792]{1,0:T(8,128)(2,1)S(1)} all-gather(bf16[16,1792]{1,0:T(8,128)(2,1)S(1)} %pad_maximum_fusion.3), channel_id=1, replica_groups=mesh['gx_0'=2,'gx_1'=8,'gy'=16] {'gx_0','gx_1'}, dimensions={0}, use_global_device_ids=true | all-gather | bytes 974848 | tf_op jit(solution)/shard_map/all_gather | solution.py:52
  260.9 0.4 fusion.9
  261.3 0.4 fusion.8
  261.8 1.3 copy.14
  263.1 1.3 copy.15
  (14 shorter events, 0.1 us)
Async XLA Ops:
  7.2 134.5 %copy-start = (bf16[896,512]{1,0:T(8,128)(2,1)S(1)}, bf16[896,512]{1,0:T(8,128)(2,1)}, u32[]{:S(2)}) copy-start(bf16[896,512]{1,0:T(8,128)(2,1)} %param.12) | copy-start | bytes 2752516
  7.2 68.6 %reduce-scatter.3.cloned.1.call-start = ((), (), s32[]{:S(2)}) async-start(), calls=%async_computation.5 | async-start | bytes 4128768 | tf_op jit(solution)/shard_map/reduce_scatter | solution.py:35
  26.2 116.4 %copy-start.1 = (bf16[896,512]{1,0:T(8,128)(2,1)S(1)}, bf16[896,512]{1,0:T(8,128)(2,1)}, u32[]{:S(2)}) copy-start(bf16[896,512]{1,0:T(8,128)(2,1)} %param.15) | copy-start | bytes 2752516
  26.2 73.2 %reduce-scatter.5.cloned.1.call-start = ((), (), s32[]{:S(2)}) async-start(), calls=%async_computation.6 | async-start | bytes 688128 | tf_op jit(solution)/shard_map/reduce_scatter | solution.py:35
  142.6 21.2 %copy-start.3 = (bf16[16,512]{1,0:T(8,128)(2,1)S(1)}, bf16[16,512]{1,0:T(8,128)(2,1)}, u32[]{:S(2)}) copy-start(bf16[16,512]{1,0:T(8,128)(2,1)} %param.9) | copy-start | bytes 49156
  163.8 19.1 %copy-start.2 = (bf16[896,512]{1,0:T(8,128)(2,1)S(1)}, bf16[896,512]{1,0:T(8,128)(2,1)}, u32[]{:S(2)}) copy-start(bf16[896,512]{1,0:T(8,128)(2,1)} %param.15) | copy-start | bytes 2752516
  184.4 33.4 %all-to-all-start.2 = ((bf16[16,16,1792]{2,1,0:T(8,128)(2,1)}), bf16[16,16,1792]{2,1,0:T(8,128)(2,1)S(1)}, u32[]{:S(2)}, u32[]{:S(2)}) async-start(bf16[16,16,1792]{2,1,0:T(8,128)(2,1)} %pad_maximum_fusion.1), calls=%async_computation.4 | async-start | bytes 1835008 | tf_op jit(solution)/shard_map/all_to_all | solution.py:67
Sparse Core Ops, SparseCore 0:
  26.3 49.4 reduce-scatter.2
  78.3 21.0 reduce-scatter.4
where the time goes:
time: 273 us; the launch traced here: 271 us
  blocking collectives  135 us (49%)
  waiting for transfers between devices  96.7 us (35%)
  between operations  14.2 us (5%)
  matrix products  8.44 us (3%)
  starting transfers between devices  8.19 us (3%)
  local copies, waits for them, and re-layouts  5.49 us (2%)
  other arithmetic  3.21 us (1%)
    all_gather x3, blocking collectives, sent_together(): filled, at, outs = (lax.all_gather(both, axis, axis=dim, tiled=True), 0, [])  101 us
    reduce_scatter x2, waiting for transfers between devices, reduced_to_own(): parts = lax.psum_scatter(parts, axes[k], scatter_dimension=0, tiled=True)  73.2 us
    all_to_all x1, waiting for transfers between devices, summed_on_arrival(): lax.all_to_all(parts, axis, split_axis=0, concat_axis=0, tiled=True)  23.5 us
    all_to_all x1, blocking collectives, sum_at_owner(): parts = lax.all_to_all(split_up(value, dim, length), axis, 0, 0, tiled=True)  20.6 us
    all_to_all x1, blocking collectives, copy_for_each(): return lax.all_to_all(copies, axis, split_axis=0, concat_axis=0, tiled=True)  12.9 us
    all_to_all x1, starting transfers between devices, summed_on_arrival(): lax.all_to_all(parts, axis, split_axis=0, concat_axis=0, tiled=True)  8.11 us
  transfers between devices with their start and end apart: 3, of which 3 were waited for; matrix products, arithmetic and copies ran while one was open for 1% of the time, Pallas kernels for 0%

commit v1 on v0

v1 whole, which is shorter than its diff:
```python
import functools
import math

import jax
import jax.numpy as jnp
from jax import lax
from jax.experimental import pallas as pl
from jax.experimental.pallas import tpu as pltpu
from jax.sharding import PartitionSpec as P

MESH = pl.DeviceIdType.MESH
TOKENS = 256
DL = 512
FL = 896
NZ = 8
NG = 16
ROWS = 32
F32 = jnp.float32
BF16 = jnp.bfloat16


def silu_parts(gate):
    sig = jax.nn.sigmoid(gate)
    first = sig * (1.0 + gate * (1.0 - sig))
    second = sig * (1.0 - sig) * (2.0 + gate * (1.0 - 2.0 * sig))
    return (gate * sig, first, second)


def lead_dot(left, right):
    return lax.dot_general(left, right, (((0,), (0,)), ((), ())), preferred_element_type=F32)


def tail_dot(left, right):
    return lax.dot_general(left, right, (((1,), (1,)), ((), ())), preferred_element_type=F32)


def kernel(
    tok, tgt, wg, wu, wd, tg, tu, td,
    x_out, ag_out, g_out,
    xs, tgv, wup, wdn, part, sbuf, rbuf, ysend, yrecv, act, ag, osum, osend, orecv, gs,
    lsem, p0s, p0r, rss, rsr, ys, yr, ags, agr, p3s, p3r, p4s, p4r,
):
    scale = 1.0 / math.sqrt(TOKENS)
    g = lax.axis_index("gx")
    h = lax.axis_index("gy")
    yh = lax.div(g, NZ)
    z = lax.rem(g, NZ)
    up_z = yh * NZ + lax.rem(z + 1, NZ)
    dn_z = yh * NZ + lax.rem(z + NZ - 1, NZ)
    pair = lax.rem(g + NZ, 2 * NZ)

    def at_gx(i):
        return {"gx": i}

    def at_gy(i):
        return {"gy": i}

    pending = []

    def send(src, dst, ssem, rsem, where):
        copy = pltpu.make_async_remote_copy(
            src_ref=src, dst_ref=dst, send_sem=ssem, recv_sem=rsem, device_id=where, device_id_type=MESH
        )
        copy.start()
        pending.append(copy)

    def arrived(dst, ssem, rsem, where):
        pltpu.make_async_remote_copy(
            src_ref=dst, dst_ref=dst, send_sem=ssem, recv_sem=rsem, device_id=where, device_id_type=MESH
        ).wait_recv()

    local = []
    own_tok = pltpu.make_async_copy(tok, xs.at[h], lsem.at[0])
    own_tok.start()
    for i, w in enumerate((wg, wu, tg, tu)):
        c = pltpu.make_async_copy(w, wup.at[i], lsem.at[1 + i])
        c.start()
        local.append(c)
    for i, w in enumerate((wd, td)):
        c = pltpu.make_async_copy(w, wdn.at[i], lsem.at[5 + i])
        c.start()
        local.append(c)
    own_tgt = pltpu.make_async_copy(tgt, tgv, lsem.at[7])
    own_tgt.start()

    barrier = pltpu.get_barrier_semaphore()
    for i in (up_z, dn_z, pair):
        pl.semaphore_signal(barrier, inc=1, device_id=at_gx(i), device_id_type=MESH)
    for k in range(1, NG):
        pl.semaphore_signal(barrier, inc=1, device_id=at_gy(lax.rem(h + k, NG)), device_id_type=MESH)
    pl.semaphore_wait(barrier, 3 + NG - 1)

    order = (8, 7, 9, 6, 10, 5, 11, 4, 12, 3, 13, 2, 14, 1, 15)
    own_tok.wait()
    for k in order:
        send(xs.at[h], xs.at[h], p0s.at[k], p0r.at[k], at_gy(lax.rem(h + k, NG)))
    for k in reversed(order):
        src = lax.rem(h + NG - k, NG)
        arrived(xs.at[src], p0s.at[k], p0r.at[k], at_gy(src))
    x_copy = pltpu.make_async_copy(xs, x_out, lsem.at[8])
    x_copy.start()

    tokens = xs[...].reshape(TOKENS, DL)

    def zrow(i):
        return pl.ds(pl.multiple_of(ROWS * lax.rem(i + NZ, NZ), ROWS), ROWS)

    def long_way(u):
        return u % 2

    def first_step(u, d):
        return 0 if d == long_way(u) else 1

    def rs_send(u, d, s):
        ahead = 4 - s
        row = zrow(z + ahead) if d == 0 else zrow(z - ahead)
        val = part[u, row, :]
        if s > first_step(u, d):
            arrived(rbuf.at[u, d, s - 1], rss.at[u, d, s - 1], rsr.at[u, d, s - 1], at_gx(dn_z if d == 0 else up_z))
            val = val + rbuf[u, d, s - 1].astype(F32)
        sbuf[u, d, s] = val.astype(BF16)
        send(sbuf.at[u, d, s], rbuf.at[u, d, s], rss.at[u, d, s], rsr.at[u, d, s], at_gx(up_z if d == 0 else dn_z))

    def rs_start(u):
        d = long_way(u)
        rs_send(u, d, 0)
        rs_send(u, 1 - d, 1)

    def rs_last(u):
        val = part[u, zrow(z), :]
        for d in range(2):
            arrived(rbuf.at[u, d, 3], rss.at[u, d, 3], rsr.at[u, d, 3], at_gx(dn_z if d == 0 else up_z))
            val = val + rbuf[u, d, 3].astype(F32)
        part[u, zrow(z), :] = val
        ysend[u] = val.astype(BF16)
        send(ysend.at[u], yrecv.at[u], ys.at[u], yr.at[u], at_gx(pair))

    def rs_result(u):
        arrived(yrecv.at[u], ys.at[u], yr.at[u], at_gx(pair))
        return part[u, zrow(z), :] + yrecv[u].astype(F32)

    def rs_middle(units):
        for s in range(1, 4):
            for u in units:
                for d in range(2):
                    if s > first_step(u, d):
                        rs_send(u, d, s)

    def ag_send(v, d, s):
        src = zrow(z - s) if d == 0 else zrow(z + s)
        if s > 0:
            ag_wait(v, d, s - 1)
        send(
            ag.at[v, src, :], ag.at[v, src, :], ags.at[v, d, s], agr.at[v, d, s],
            at_gx(up_z if d == 0 else dn_z),
        )

    def ag_wait(v, d, s):
        src = zrow(z - 1 - s) if d == 0 else zrow(z + 1 + s)
        arrived(ag.at[v, src, :], ags.at[v, d, s], agr.at[v, d, s], at_gx(dn_z if d == 0 else up_z))

    def ag_start(v):
        for d in range(2):
            ag_send(v, d, 0)

    def ag_finish(units):
        for s in range(1, 4):
            for v in units:
                for d in range(2):
                    if s < 3 or d == long_way(v):
                        ag_send(v, d, s)
        for v in units:
            for d in range(2):
                ag_wait(v, d, 3 if d == long_way(v) else 2)

    for u in range(4):
        local[u].wait()
        for n in range(0, FL, 256):
            m = min(256, FL - n)
            part[u, :, n : n + m] = jnp.dot(tokens, wup[u, :, n : n + m], preferred_element_type=F32)
        rs_start(u)
    rs_middle(range(4))
    for u in range(4):
        rs_last(u)
    gate, upper = rs_result(0), rs_result(1)
    silu_val, first, second = silu_parts(gate)
    ag[0, zrow(z), :] = (silu_val * upper).astype(BF16)
    ag_start(0)
    gate_dot, upper_dot = rs_result(2), rs_result(3)
    ag[1, zrow(z), :] = (first * gate_dot * upper + silu_val * upper_dot).astype(BF16)
    ag_start(1)
    act[0] = gate
    act[1] = upper
    act[2] = gate_dot
    act[3] = upper_dot
    for c in local[4:]:
        c.wait()
    ag_finish((0, 1))

    def out_send(w):
        for k in order:
            dst = lax.rem(h + k, NG)
            send(osend.at[w, dst], orecv.at[w, k], p3s.at[w, k], p3r.at[w, k], at_gy(dst))

    def out_sum(w):
        total = osum[w, h]
        for k in reversed(order):
            arrived(orecv.at[w, k], p3s.at[w, k], p3r.at[w, k], at_gy(lax.rem(h + NG - k, NG)))
            total = total + orecv[w, k].astype(F32)
        return total

    def grad_send(w):
        for k in order:
            send(gs.at[w, h], gs.at[w, h], p4s.at[w, k], p4r.at[w, k], at_gy(lax.rem(h + k, NG)))

    def grad_wait(w):
        for k in reversed(order):
            src = lax.rem(h + NG - k, NG)
            arrived(gs.at[w, src], p4s.at[w, k], p4r.at[w, k], at_gy(src))

    for w in range(2):
        for n in range(0, DL, 256):
            if w == 0:
                val = jnp.dot(ag[0], wdn[0, :, n : n + 256], preferred_element_type=F32)
            else:
                val = jnp.dot(ag[1], wdn[0, :, n : n + 256], preferred_element_type=F32)
                val = val + jnp.dot(ag[0], wdn[1, :, n : n + 256], preferred_element_type=F32)
            val = val.reshape(NG, TOKENS // NG, 256)
            osum[w, :, :, n : n + 256] = val
            osend[w, :, :, n : n + 256] = val.astype(BF16)
        out_send(w)
    own_tgt.wait()
    gs[0, h] = ((out_sum(0) - tgv[...].astype(F32)) * scale).astype(BF16)
    grad_send(0)
    gs[1, h] = (out_sum(1) * scale).astype(BF16)
    grad_send(1)

    def back_part(w):
        for n in range(0, FL, 256):
            m = min(256, FL - n)
            if w == 0:
                val = tail_dot(gs[0].reshape(TOKENS, DL), wdn[0, n : n + m, :])
            else:
                val = tail_dot(gs[1].reshape(TOKENS, DL), wdn[0, n : n + m, :])
                val = val + tail_dot(gs[0].reshape(TOKENS, DL), wdn[1, n : n + m, :])
            part[4 + w, :, n : n + m] = val

    for w in range(2):
        grad_wait(w)
        back_part(w)
        rs_start(4 + w)
    rs_middle((4, 5))
    g_copy = pltpu.make_async_copy(gs, g_out, lsem.at[9])
    g_copy.start()
    for u in (4, 5):
        rs_last(u)
    gate, upper, gate_dot, upper_dot = act[0], act[1], act[2], act[3]
    silu_val, first, second = silu_parts(gate)
    back = rs_result(4)
    back_dot = rs_result(5)
    ag[2, zrow(z), :] = (
        back_dot * upper * first + back * upper_dot * first + back * upper * second * gate_dot
    ).astype(BF16)
    ag_start(2)
    ag[3, zrow(z), :] = (back_dot * silu_val + back * first * gate_dot).astype(BF16)
    ag_start(3)
    ag_finish((2, 3))
    ag_copy = pltpu.make_async_copy(ag, ag_out, lsem.at[10])
    ag_copy.start()
    for c in pending:
        c.wait_send()
    x_copy.wait()
    g_copy.wait()
    ag_copy.wait()


def body(tokens, target, w_gate, w_up, w_down, t_gate, t_up, t_down):
    any_spec = pl.BlockSpec(memory_space=pl.ANY)
    blk = TOKENS // NG
    dma = pltpu.SemaphoreType.DMA
    xfull, ag, gs = pl.pallas_call(
        kernel,
        out_shape=(
            jax.ShapeDtypeStruct((NG, blk, DL), BF16),
            jax.ShapeDtypeStruct((4, TOKENS, FL), BF16),
            jax.ShapeDtypeStruct((2, NG, blk, DL), BF16),
        ),
        in_specs=[any_spec] * 8,
        out_specs=(any_spec,) * 3,
        scratch_shapes=[
            pltpu.VMEM((NG, blk, DL), BF16),
            pltpu.VMEM((blk, DL), BF16),
            pltpu.VMEM((4, DL, FL), BF16),
            pltpu.VMEM((2, FL, DL), BF16),
            pltpu.VMEM((6, TOKENS, FL), F32),
            pltpu.VMEM((6, 2, 4, ROWS, FL), BF16),
            pltpu.VMEM((6, 2, 4, ROWS, FL), BF16),
            pltpu.VMEM((6, ROWS, FL), BF16),
            pltpu.VMEM((6, ROWS, FL), BF16),
            pltpu.VMEM((4, ROWS, FL), F32),
            pltpu.VMEM((4, TOKENS, FL), BF16),
            pltpu.VMEM((2, NG, blk, DL), F32),
            pltpu.VMEM((2, NG, blk, DL), BF16),
            pltpu.VMEM((2, NG, blk, DL), BF16),
            pltpu.VMEM((2, NG, blk, DL), BF16),
            dma((11,)),
            dma((NG,)), dma((NG,)),
            dma((6, 2, 4)), dma((6, 2, 4)),
            dma((6,)), dma((6,)),
            dma((4, 2, 4)), dma((4, 2, 4)),
            dma((2, NG)), dma((2, NG)),
            dma((2, NG)), dma((2, NG)),
        ],
        compiler_params=pltpu.CompilerParams(
            collective_id=0, has_side_effects=True, vmem_limit_bytes=40 * 1024 * 1024
        ),
    )(tokens, target, w_gate, w_up, w_down, t_gate, t_up, t_down)
    xfull = xfull.reshape(TOKENS, DL)
    gs = gs.reshape(2, TOKENS, DL)
    hvp_down = (lead_dot(ag[1], gs[0]) + lead_dot(ag[0], gs[1])).astype(BF16)
    hvp_gate = lead_dot(xfull, ag[2]).astype(BF16)
    hvp_up = lead_dot(xfull, ag[3]).astype(BF16)
    return (hvp_gate, hvp_up, hvp_down)


def solution(mesh):
    in_specs = (
        P("gy", "gx"),
        P("gy", "gx"),
        P("gx", "gy"),
        P("gx", "gy"),
        P("gy", "gx"),
        P("gx", "gy"),
        P("gx", "gy"),
        P("gy", "gx"),
    )
    out_specs = (P("gx", "gy"), P("gx", "gy"), P("gy", "gx"))
    return jax.shard_map(body, mesh=mesh, in_specs=in_specs, out_specs=out_specs, check_vma=False)
```

time: 273 us -> 120 us (0.44)
  blocking collectives: 135 us -> 0 us
  Pallas kernels: 0 us -> 106 us
  waiting for transfers between devices: 96.7 us -> 0 us
  between operations: 14.2 us -> 0.67 us
  starting transfers between devices: 8.19 us -> 0 us
  matrix products: 8.44 us -> 4.57 us
  other arithmetic: 3.21 us -> 0 us
  local copies, waits for them, and re-layouts: 5.49 us -> 8.53 us
    pallas_call x0 -> x1, Pallas kernels: none -> 106 us  [body(): pl.pallas_call(kernel, out_shape=(jax.ShapeDtypeStruct((NG, blk, DL), BF1...]
    all_gather x3 -> x0, blocking collectives: 101 us -> none  [sent_together(): filled, at, outs = (lax.all_gather(both, axis, axis=dim, tiled=True), 0, [])]
    reduce_scatter x2 -> x0, waiting for transfers between devices: 73.2 us -> none  [reduced_to_own(): parts = lax.psum_scatter(parts, axes[k], scatter_dimension=0, tiled=True)]
    all_to_all x2 -> x0, blocking collectives: 33.5 us -> none  [the longest x1 20.6 us: sum_at_owner(): parts = lax.all_to_all(split_up(value, dim, length), axis, 0, 0, tiled=True)]
    all_to_all x1 -> x0, waiting for transfers between devices: 23.5 us -> none  [summed_on_arrival(): lax.all_to_all(parts, axis, split_axis=0, concat_axis=0, tiled=True)]
    all_to_all x1 -> x0, starting transfers between devices: 8.11 us -> none  [summed_on_arrival(): lax.all_to_all(parts, axis, split_axis=0, concat_axis=0, tiled=True)]
    unnamed x10 -> x16, local copies, waits for them, and re-layouts: 2.57 us -> 8.5 us
    dot_general x7 -> x0, matrix products: 5.81 us -> none  [the longest x4 4.41 us: matmul(): return jnp.dot(left, right, preferred_element_type=jnp.float32)]
  transfers between devices with their start and end apart: 3 -> 0, of which waited for: 3 -> 0; matrix products, arithmetic and copies ran while one was open for 1% -> 0% of each run, Pallas kernels for 0% -> 0%
where the time goes in v1:
time: 120 us
  Pallas kernels  106 us (88%)
  local copies, waits for them, and re-layouts  8.53 us (7%)
  matrix products  4.57 us (4%)
    pallas_call x1, Pallas kernels, body(): pl.pallas_call(kernel, out_shape=(jax.ShapeDtypeStruct((NG, blk, DL), BF1...  106 us
    unnamed x16, local copies, waits for them, and re-layouts  8.5 us
    dot_general x4, matrix products, lead_dot(): lax.dot_general(left, right, (((0,), (0,)), ((), ())), preferred_element_...  4.57 us

profile of v1, /device:TPU:32, one launch (start us, length us, event | category | flops | bytes accessed | tf_op | source)
XLA Modules:
  0.0 119.5 jit_solution(15323078634185501971)
XLA Ops:
  0.6 0.0 copy-start
  0.6 1.2 copy-done
  1.8 0.0 copy-start.1
  1.8 1.2 copy-done.1
  3.0 0.0 copy-start.2
  3.0 1.2 copy-done.2
  4.2 0.0 copy-start.3
  4.2 1.2 copy-done.3
  5.4 0.0 copy-start.4
  5.4 1.2 copy-done.4
  6.5 0.0 copy-start.5
  6.5 1.2 copy-done.5
  7.7 0.0 copy-start.6
  7.7 0.7 copy-done.6
  8.4 0.0 copy-start.7
  8.4 0.7 copy-done.7
  9.1 105.7 %shard_map.103 = (bf16[16,16,512]{2,1,0:T(8,128)(2,1)S(1)}, bf16[4,256,896]{2,1,0:T(8,128)(2,1)S(1)}, bf16[2,16,16,512]{3,2,1,0:T(8,128)(2,1)S(1)}) custom-call(bf16[16,512]{1,0:T(8,128)(2,1)S(1)} %copy-done.6, bf16[16,512]{1,0:T(8,128)(2,1)S(1)} %copy-done.7, bf16[512,896]{1,0:T(8,128)(2,1)S(1)} %copy-done, bf16[512,896]{1,0:T(8,128)(2,1)S(1)} %copy-done.1, ...), custom_call_target="tpu_custom_call" | custom-call | tf_op jit(solution)/shard_map/pallas_call | solution.py:281
  114.9 0.4 fusion.1
  115.4 1.4 %add_convert_fusion = bf16[896,512]{1,0:T(8,128)(2,1)} fusion(f32[896,512]{1,0:T(8,128)S(1)} %fusion.1, bf16[256,512]{1,0:T(8,128)(2,1)S(1)} %bitcast.22, bf16[4,256,896]{2,1,0:T(8,128)(2,1)S(1)} %get-tuple-element.7), kind=kOutput, calls=%fused_computation | convolution fusion | flops 235798528 | bytes 3473408 | tf_op jit(solution)/shard_map/dot_general | solution.py:30
  116.7 1.4 %convolution_convert_fusion = bf16[512,896]{1,0:T(8,128)(2,1)} fusion(bf16[256,512]{1,0:T(8,128)(2,1)S(1)} %bitcast.19, bf16[4,256,896]{2,1,0:T(8,128)(2,1)S(1)} %get-tuple-element.7), kind=kOutput, calls=%fused_computation.1 | convolution fusion | flops 235339776 | bytes 1638400 | tf_op jit(solution)/shard_map/dot_general | solution.py:30
  118.1 1.4 %convolution_convert_fusion.1 = bf16[512,896]{1,0:T(8,128)(2,1)} fusion(bf16[256,512]{1,0:T(8,128)(2,1)S(1)} %bitcast.20, bf16[4,256,896]{2,1,0:T(8,128)(2,1)S(1)} %get-tuple-element.7), kind=kOutput, calls=%fused_computation.2 | convolution fusion | flops 235339776 | bytes 1638400 | tf_op jit(solution)/shard_map/dot_general | solution.py:30
  (1 shorter events, 0.0 us)
Async XLA Ops:
  0.6 1.2 copy-start
  1.8 1.2 copy-start.1
  3.0 1.2 copy-start.2
  4.2 1.2 copy-start.3
  5.4 1.2 copy-start.4
  6.5 1.2 copy-start.5
  7.7 0.7 copy-start.6
  8.4 0.7 copy-start.7

commit v2 on v1

--- a/solution.py
+++ b/solution.py
@@ -34,15 +34,38 @@
     return lax.dot_general(left, right, (((1,), (1,)), ((), ())), preferred_element_type=F32)
 
 
+def encode2(v):
+    return (v * jnp.abs(v)).astype(BF16)
+
+
+def decode2(c):
+    v = c.astype(F32)
+    root = jnp.sqrt(jnp.abs(v))
+    return jnp.where(v < 0.0, -root, root)
+
+
+def encode4(v):
+    return (v * jnp.abs(v) * (v * v)).astype(BF16)
+
+
+def decode4(c):
+    v = c.astype(F32)
+    root = jnp.sqrt(jnp.sqrt(jnp.abs(v)))
+    return jnp.where(v < 0.0, -root, root)
+
+
 def kernel(
     tok, tgt, wg, wu, wd, tg, tu, td,
-    x_out, ag_out, g_out,
-    xs, tgv, wup, wdn, part, sbuf, rbuf, ysend, yrecv, act, ag, osum, osend, orecv, gs,
-    lsem, p0s, p0r, rss, rsr, ys, yr, ags, agr, p3s, p3r, p4s, p4r,
+    xt_out, ag_out, hd_out,
+    xs, tgv, wup, wdn, part, sbuf, rbuf, ysend, yrecv, act, ag, osum, osend, ocore, orecv, gs,
+    lsem, p0s, p0r, rss, rsr, ys, yr, ags, agr, p3s, p3r, p4s, p4r, ds, dr,
 ):
     scale = 1.0 / math.sqrt(TOKENS)
     g = lax.axis_index("gx")
     h = lax.axis_index("gy")
+    core = lax.rem(h, 2)
+    mine = lax.div(h, 2)
+    mate = h + 1 - 2 * core
     yh = lax.div(g, NZ)
     z = lax.rem(g, NZ)
     up_z = yh * NZ + lax.rem(z + 1, NZ)
@@ -56,6 +79,12 @@
         return {"gy": i}
 
     pending = []
+
+    def enc(u, v):
+        return encode4(v) if u < 4 else encode2(v)
+
+    def dec(u, v):
+        return decode4(v) if u < 4 else decode2(v)
 
     def send(src, dst, ssem, rsem, where):
         copy = pltpu.make_async_remote_copy(
@@ -68,6 +97,23 @@
         pltpu.make_async_remote_copy(
             src_ref=dst, dst_ref=dst, send_sem=ssem, recv_sem=rsem, device_id=where, device_id_type=MESH
         ).wait_recv()
+
+    far = (4, 5, 3, 6, 2, 7, 1)
+
+    def spread(ref, ssem, rsem):
+        for k in far:
+            send(ref.at[h], ref.at[h], ssem.at[k], rsem.at[k], at_gy(lax.rem(h + 2 * k, NG)))
+        send(ref.at[h], ref.at[h], ssem.at[8], rsem.at[8], at_gy(mate))
+
+    def collect(ref, ssem, rsem):
+        for k in reversed(far):
+            src = lax.rem(h + NG - 2 * k, NG)
+            arrived(ref.at[src], ssem.at[k], rsem.at[k], at_gy(src))
+            send(ref.at[src], ref.at[src], ssem.at[8 + k], rsem.at[8 + k], at_gy(mate))
+        arrived(ref.at[mate], ssem.at[8], rsem.at[8], at_gy(mate))
+        for k in reversed(far):
+            src = lax.rem(mate + NG - 2 * k, NG)
+            arrived(ref.at[src], ssem.at[8 + k], rsem.at[8 + k], at_gy(mate))
 
     local = []
     own_tok = pltpu.make_async_copy(tok, xs.at[h], lsem.at[0])
@@ -86,19 +132,14 @@
     barrier = pltpu.get_barrier_semaphore()
     for i in (up_z, dn_z, pair):
         pl.semaphore_signal(barrier, inc=1, device_id=at_gx(i), device_id_type=MESH)
-    for k in range(1, NG):
-        pl.semaphore_signal(barrier, inc=1, device_id=at_gy(lax.rem(h + k, NG)), device_id_type=MESH)
-    pl.semaphore_wait(barrier, 3 + NG - 1)
-
-    order = (8, 7, 9, 6, 10, 5, 11, 4, 12, 3, 13, 2, 14, 1, 15)
+    for k in range(1, 8):
+        pl.semaphore_signal(barrier, inc=1, device_id=at_gy(lax.rem(h + 2 * k, NG)), device_id_type=MESH)
+    pl.semaphore_signal(barrier, inc=1, device_id=at_gy(mate), device_id_type=MESH)
+    pl.semaphore_wait(barrier, 11)
+
     own_tok.wait()
-    for k in order:
-        send(xs.at[h], xs.at[h], p0s.at[k], p0r.at[k], at_gy(lax.rem(h + k, NG)))
-    for k in reversed(order):
-        src = lax.rem(h + NG - k, NG)
-        arrived(xs.at[src], p0s.at[k], p0r.at[k], at_gy(src))
-    x_copy = pltpu.make_async_copy(xs, x_out, lsem.at[8])
-    x_copy.start()
+    spread(xs, p0s, p0r)
+    collect(xs, p0s, p0r)
 
     tokens = xs[...].reshape(TOKENS, DL)
 
@@ -117,8 +158,8 @@
         val = part[u, row, :]
         if s > first_step(u, d):
             arrived(rbuf.at[u, d, s - 1], rss.at[u, d, s - 1], rsr.at[u, d, s - 1], at_gx(dn_z if d == 0 else up_z))
-            val = val + rbuf[u, d, s - 1].astype(F32)
-        sbuf[u, d, s] = val.astype(BF16)
+            val = val + dec(u, rbuf[u, d, s - 1])
+        sbuf[u, d, s] = enc(u, val)
         send(sbuf.at[u, d, s], rbuf.at[u, d, s], rss.at[u, d, s], rsr.at[u, d, s], at_gx(up_z if d == 0 else dn_z))
 
     def rs_start(u):
@@ -130,14 +171,14 @@
         val = part[u, zrow(z), :]
         for d in range(2):
             arrived(rbuf.at[u, d, 3], rss.at[u, d, 3], rsr.at[u, d, 3], at_gx(dn_z if d == 0 else up_z))
-            val = val + rbuf[u, d, 3].astype(F32)
+            val = val + dec(u, rbuf[u, d, 3])
         part[u, zrow(z), :] = val
-        ysend[u] = val.astype(BF16)
+        ysend[u] = enc(u, val)
         send(ysend.at[u], yrecv.at[u], ys.at[u], yr.at[u], at_gx(pair))
 
     def rs_result(u):
         arrived(yrecv.at[u], ys.at[u], yr.at[u], at_gx(pair))
-        return part[u, zrow(z), :] + yrecv[u].astype(F32)
+        return part[u, zrow(z), :] + dec(u, yrecv[u])
 
     def rs_middle(units):
         for s in range(1, 4):
@@ -179,6 +220,7 @@
             m = min(256, FL - n)
             part[u, :, n : n + m] = jnp.dot(tokens, wup[u, :, n : n + m], preferred_element_type=F32)
         rs_start(u)
+    xt_out[...] = tokens.T
     rs_middle(range(4))
     for u in range(4):
         rs_last(u)
@@ -197,43 +239,40 @@
         c.wait()
     ag_finish((0, 1))
 
-    def out_send(w):
-        for k in order:
-            dst = lax.rem(h + k, NG)
-            send(osend.at[w, dst], orecv.at[w, k], p3s.at[w, k], p3r.at[w, k], at_gy(dst))
-
-    def out_sum(w):
-        total = osum[w, h]
-        for k in reversed(order):
-            arrived(orecv.at[w, k], p3s.at[w, k], p3r.at[w, k], at_gy(lax.rem(h + NG - k, NG)))
-            total = total + orecv[w, k].astype(F32)
-        return total
-
-    def grad_send(w):
-        for k in order:
-            send(gs.at[w, h], gs.at[w, h], p4s.at[w, k], p4r.at[w, k], at_gy(lax.rem(h + k, NG)))
-
-    def grad_wait(w):
-        for k in reversed(order):
-            src = lax.rem(h + NG - k, NG)
-            arrived(gs.at[w, src], p4s.at[w, k], p4r.at[w, k], at_gy(src))
-
-    for w in range(2):
+    def out_part(w):
         for n in range(0, DL, 256):
             if w == 0:
                 val = jnp.dot(ag[0], wdn[0, :, n : n + 256], preferred_element_type=F32)
             else:
                 val = jnp.dot(ag[1], wdn[0, :, n : n + 256], preferred_element_type=F32)
                 val = val + jnp.dot(ag[0], wdn[1, :, n : n + 256], preferred_element_type=F32)
-            val = val.reshape(NG, TOKENS // NG, 256)
-            osum[w, :, :, n : n + 256] = val
-            osend[w, :, :, n : n + 256] = val.astype(BF16)
-        out_send(w)
+            osum[w, :, :, :, n : n + 256] = val.reshape(8, 2, TOKENS // NG, 256)
+        osend[w, 0] = encode2(osum[w, :, 1 - core])
+        send(osend.at[w, 0], ocore.at[w], ds.at[w], dr.at[w], at_gy(mate))
+
+    def out_send(w):
+        arrived(ocore.at[w], ds.at[w], dr.at[w], at_gy(mate))
+        for k in far:
+            dst = lax.rem(mine + k, 8)
+            osend[w, 1, k] = encode2(osum[w, dst, core] + decode2(ocore[w, dst]))
+            send(osend.at[w, 1, k], orecv.at[w, k], p3s.at[w, k], p3r.at[w, k], at_gy(2 * dst + core))
+
+    def out_sum(w):
+        total = osum[w, mine, core] + decode2(ocore[w, mine])
+        for k in reversed(far):
+            arrived(orecv.at[w, k], p3s.at[w, k], p3r.at[w, k], at_gy(lax.rem(h + NG - 2 * k, NG)))
+            total = total + decode2(orecv[w, k])
+        return total
+
+    out_part(0)
+    out_part(1)
+    out_send(0)
+    out_send(1)
     own_tgt.wait()
     gs[0, h] = ((out_sum(0) - tgv[...].astype(F32)) * scale).astype(BF16)
-    grad_send(0)
+    spread(gs.at[0], p4s.at[0], p4r.at[0])
     gs[1, h] = (out_sum(1) * scale).astype(BF16)
-    grad_send(1)
+    spread(gs.at[1], p4s.at[1], p4r.at[1])
 
     def back_part(w):
         for n in range(0, FL, 256):
@@ -245,13 +284,17 @@
                 val = val + tail_dot(gs[0].reshape(TOKENS, DL), wdn[1, n : n + m, :])
             part[4 + w, :, n : n + m] = val
 
+    def down_part(n):
+        g0 = gs[0, :, :, n : n + 256].reshape(TOKENS, 256)
+        g1 = gs[1, :, :, n : n + 256].reshape(TOKENS, 256)
+        hd_out[:, n : n + 256] = (lead_dot(ag[1], g0) + lead_dot(ag[0], g1)).astype(BF16)
+
     for w in range(2):
-        grad_wait(w)
+        collect(gs.at[w], p4s.at[w], p4r.at[w])
         back_part(w)
         rs_start(4 + w)
+    down_part(0)
     rs_middle((4, 5))
-    g_copy = pltpu.make_async_copy(gs, g_out, lsem.at[9])
-    g_copy.start()
     for u in (4, 5):
         rs_last(u)
     gate, upper, gate_dot, upper_dot = act[0], act[1], act[2], act[3]
@@ -264,29 +307,47 @@
     ag_start(2)
     ag[3, zrow(z), :] = (back_dot * silu_val + back * first * gate_dot).astype(BF16)
     ag_start(3)
+    down_part(256)
     ag_finish((2, 3))
-    ag_copy = pltpu.make_async_copy(ag, ag_out, lsem.at[10])
+    ag_copy = pltpu.make_async_copy(ag.at[pl.ds(2, 2)], ag_out, lsem.at[8])
     ag_copy.start()
     for c in pending:
         c.wait_send()
-    x_copy.wait()
-    g_copy.wait()
     ag_copy.wait()
 
 
-def body(tokens, target, w_gate, w_up, w_down, t_gate, t_up, t_down):
-    any_spec = pl.BlockSpec(memory_space=pl.ANY)
+def weights_kernel(xt, ag, hd, gate_out, up_out, down_out, buf, sem):
+    rows = DL // 4
+    down = pltpu.make_async_copy(hd, down_out, sem.at[8])
+    down.start()
+    copies = []
+    for v, out in enumerate((gate_out, up_out)):
+        for i in range(4):
+            part = pl.ds(i * rows, rows)
+            buf[v, part, :] = jnp.dot(xt[part, :], ag[v], preferred_element_type=F32).astype(BF16)
+            copy = pltpu.make_async_copy(buf.at[v, part, :], out.at[part, :], sem.at[4 * v + i])
+            copy.start()
+            copies.append(copy)
+    down.wait()
+    for copy in copies:
+        copy.wait()
+
+
+def body(*args):
+    hbm = pl.BlockSpec(memory_space=pltpu.HBM)
+    vmem = pl.BlockSpec(memory_space=pltpu.VMEM)
     blk = TOKENS // NG
     dma = pltpu.SemaphoreType.DMA
-    xfull, ag, gs = pl.pallas_call(
+    args = [pltpu.with_memory_space_constraint(a, pltpu.HBM) for a in args]
+    xt, ag, hd = pl.pallas_call(
         kernel,
         out_shape=(
-            jax.ShapeDtypeStruct((NG, blk, DL), BF16),
-            jax.ShapeDtypeStruct((4, TOKENS, FL), BF16),
-            jax.ShapeDtypeStruct((2, NG, blk, DL), BF16),
+            jax.ShapeDtypeStruct((DL, TOKENS), BF16),
+            jax.ShapeDtypeStruct((2, TOKENS, FL), BF16),
+            jax.ShapeDtypeStruct((FL, DL), BF16),
         ),
-        in_specs=[any_spec] * 8,
-        out_specs=(any_spec,) * 3,
+        in_specs=[hbm] * 8,
+        out_specs=(vmem, pl.BlockSpec(memory_space=pl.ANY), vmem),
         scratch_shapes=[
             pltpu.VMEM((NG, blk, DL), BF16),
             pltpu.VMEM((blk, DL), BF16),
@@ -299,28 +360,36 @@
             pltpu.VMEM((6, ROWS, FL), BF16),
             pltpu.VMEM((4, ROWS, FL), F32),
             pltpu.VMEM((4, TOKENS, FL), BF16),
-            pltpu.VMEM((2, NG, blk, DL), F32),
+            pltpu.VMEM((2, 8, 2, blk, DL), F32),
+            pltpu.VMEM((2, 2, 8, blk, DL), BF16),
+            pltpu.VMEM((2, 8, blk, DL), BF16),
+            pltpu.VMEM((2, 8, blk, DL), BF16),
             pltpu.VMEM((2, NG, blk, DL), BF16),
-            pltpu.VMEM((2, NG, blk, DL), BF16),
-            pltpu.VMEM((2, NG, blk, DL), BF16),
-            dma((11,)),
+            dma((9,)),
             dma((NG,)), dma((NG,)),
             dma((6, 2, 4)), dma((6, 2, 4)),
             dma((6,)), dma((6,)),
             dma((4, 2, 4)), dma((4, 2, 4)),
+            dma((2, 8)), dma((2, 8)),
             dma((2, NG)), dma((2, NG)),
-            dma((2, NG)), dma((2, NG)),
+            dma((2,)), dma((2,)),
         ],
         compiler_params=pltpu.CompilerParams(
             collective_id=0, has_side_effects=True, vmem_limit_bytes=40 * 1024 * 1024
         ),
-    )(tokens, target, w_gate, w_up, w_down, t_gate, t_up, t_down)
-    xfull = xfull.reshape(TOKENS, DL)
-    gs = gs.reshape(2, TOKENS, DL)
-    hvp_down = (lead_dot(ag[1], gs[0]) + lead_dot(ag[0], gs[1])).astype(BF16)
-    hvp_gate = lead_dot(xfull, ag[2]).astype(BF16)
-    hvp_up = lead_dot(xfull, ag[3]).astype(BF16)
-    return (hvp_gate, hvp_up, hvp_down)
+    )(*args)
+    return pl.pallas_call(
+        weights_kernel,
+        out_shape=(
+            jax.ShapeDtypeStruct((DL, FL), BF16),
+            jax.ShapeDtypeStruct((DL, FL), BF16),
+            jax.ShapeDtypeStruct((FL, DL), BF16),
+        ),
+        in_specs=[vmem] * 3,
+        out_specs=(hbm,) * 3,
+        scratch_shapes=[pltpu.VMEM((2, DL, FL), BF16), dma((9,))],
+        compiler_params=pltpu.CompilerParams(vmem_limit_bytes=16 * 1024 * 1024),
+    )(xt, ag, hd)
 
 
 def solution(mesh):

time: 120 us -> 108 us (0.900)
  local copies, waits for them, and re-layouts: 8.53 us -> 0 us
  matrix products: 4.57 us -> 0 us
    unnamed x16 -> x0, local copies, waits for them, and re-layouts: 8.5 us -> none
    dot_general x4 -> x0, matrix products: 4.57 us -> none  [lead_dot(): lax.dot_general(left, right, (((0,), (0,)), ((), ())), preferred_element_...]
    pallas_call x1 -> x2, Pallas kernels: 106 us -> 107 us  [the longest x1 105 us: body(): pl.pallas_call(kernel, out_shape=(jax.ShapeDtypeStruct((DL, TOKENS), BF16...]
where the time goes in v2:
time: 108 us
  Pallas kernels  107 us (99%)
    pallas_call x1, Pallas kernels, body(): pl.pallas_call(kernel, out_shape=(jax.ShapeDtypeStruct((DL, TOKENS), BF16...  105 us

profile of v2, /device:TPU:32, one launch (start us, length us, event | category | flops | bytes accessed | tf_op | source)
XLA Modules:
  0.0 107.7 jit_solution(5565237208840654997)
XLA Ops:
  0.6 105.4 %shard_map.103 = (bf16[512,256]{1,0:T(8,128)(2,1)S(1)}, bf16[2,256,896]{2,1,0:T(8,128)(2,1)S(1)}, bf16[896,512]{1,0:T(8,128)(2,1)S(1)}) custom-call(bf16[16,512]{1,0:T(8,128)(2,1)} %tok.1, bf16[16,512]{1,0:T(8,128)(2,1)} %tgt.1, bf16[512,896]{1,0:T(8,128)(2,1)} %wg.1, bf16[512,896]{1,0:T(8,128)(2,1)} %wu.1, bf16[896,512]{1,0:T(8,128)(2,1)} %wd.1, ...), custom_call_target="tpu_custom_call" | custom-call | tf_op jit(solution)/shard_map/pallas_call | solution.py:342
  106.1 1.6 %shard_map.104 = (bf16[512,896]{1,0:T(8,128)(2,1)}, bf16[512,896]{1,0:T(8,128)(2,1)}, bf16[896,512]{1,0:T(8,128)(2,1)}) custom-call(bf16[512,256]{1,0:T(8,128)(2,1)S(1)} %get-tuple-element.6.xt, bf16[2,256,896]{2,1,0:T(8,128)(2,1)S(1)} %get-tuple-element.7.ag, bf16[896,512]{1,0:T(8,128)(2,1)S(1)} %get-tuple-element.8.hd), custom_call_target="tpu_custom_call" | custom-call | tf_op jit(solution)/shard_map/pallas_call | solution.py:381

commit v3 on v0

v3 whole, which is shorter than its diff:
```python
import functools
import math

import jax
import jax.numpy as jnp
from jax import lax
from jax.experimental import pallas as pl
from jax.experimental.pallas import tpu as pltpu
from jax.sharding import PartitionSpec as P

MESH = pl.DeviceIdType.MESH
TOKENS = 256
DL = 512
FL = 896
NZ = 8
NG = 16
F32 = jnp.float32
BF16 = jnp.bfloat16


def silu_parts(gate):
    sig = jax.nn.sigmoid(gate)
    first = sig * (1.0 + gate * (1.0 - sig))
    second = sig * (1.0 - sig) * (2.0 + gate * (1.0 - 2.0 * sig))
    return (gate * sig, first, second)


def lead_dot(left, right):
    return lax.dot_general(left, right, (((0,), (0,)), ((), ())), preferred_element_type=F32)


def tail_dot(left, right):
    return lax.dot_general(left, right, (((1,), (1,)), ((), ())), preferred_element_type=F32)


def encode2(v):
    return (v * jnp.abs(v)).astype(BF16)


def decode2(c):
    v = c.astype(F32)
    root = jnp.sqrt(jnp.abs(v))
    return jnp.where(v < 0.0, -root, root)


def encode4(v):
    return (v * jnp.abs(v) * (v * v)).astype(BF16)


def decode4(c):
    v = c.astype(F32)
    root = jnp.sqrt(jnp.sqrt(jnp.abs(v)))
    return jnp.where(v < 0.0, -root, root)


def kernel(
    tok, tgt, wg, wu, wd, tg, tu, td,
    xt_out, ag_out, hd_out,
    xs, xt, hd, tgv, wup, wdn, part, sbuf, rbuf, pbuf, fin, act, ag, osum, osend, ocore, oown, orecv, gs,
    lsem, xsem, rss, pss, rsr, fsr, ags, agr, oss, osr, gss, gsr,
):
    scale = 1.0 / math.sqrt(TOKENS)
    g = lax.axis_index("gx")
    h = lax.axis_index("gy")
    core = lax.rem(h, 2)
    mine = lax.div(h, 2)
    mate = h + 1 - 2 * core
    yh = lax.div(g, NZ)
    z = lax.rem(g, NZ)
    own8 = pl.ds(pl.multiple_of(64 * core + 8 * mine, 8), 8)
    core64 = pl.ds(pl.multiple_of(64 * core, 64), 64)
    zown = pl.ds(pl.multiple_of(16 * z + 8 * yh, 8), 8)

    def zat(k):
        return lax.rem(z + k + NZ, NZ)

    def column(k, other=False):
        y = 1 - yh if other else yh
        return {"gx": y * NZ + zat(k)}

    def at_gy(i):
        return {"gy": i}

    def way(d, k):
        return k if d == 0 else -k

    def send(src, dst, ssem, rsem, where):
        pltpu.make_async_remote_copy(
            src_ref=src, dst_ref=dst, send_sem=ssem, recv_sem=rsem, device_id=where, device_id_type=MESH
        ).start()

    def arrived(ref, sem):
        pltpu.make_async_remote_copy(
            src_ref=ref, dst_ref=ref, send_sem=sem, recv_sem=sem, device_id=at_gy(mate), device_id_type=MESH
        ).wait_recv()

    def left(ref, sem):
        pltpu.make_async_remote_copy(
            src_ref=ref, dst_ref=ref, send_sem=sem, recv_sem=sem, device_id=at_gy(mate), device_id_type=MESH
        ).wait_send()

    def local_copy(src, dst, i):
        copy = pltpu.make_async_copy(src, dst, lsem.at[i])
        copy.start()
        return copy

    own_tok = [local_copy(tok.at[pl.ds(8 * t, 8), :], xs.at[t, own8, :], t) for t in range(2)]
    local = [local_copy(w, wup.at[i], 2 + i) for i, w in enumerate((wg, wu, tg, tu))]
    local += [local_copy(w, wdn.at[i], 6 + i) for i, w in enumerate((wd, td))]
    own_tgt = local_copy(tgt, tgv, 8)

    with jax.named_scope("barrier"):
        barrier = pltpu.get_barrier_semaphore()
        near = [column(k, o) for k in (1, -1, 2, -2) for o in (False, True)] + [column(0, True)]
        near += [at_gy(lax.rem(h + 2 * k, NG)) for k in range(1, 8)] + [at_gy(mate)]
        for where in near:
            pl.semaphore_signal(barrier, inc=1, device_id=where, device_id_type=MESH)
        pl.semaphore_wait(barrier, len(near))

    far = (4, 5, 3, 6, 2, 7, 1)

    def spread(block, ssem, rsem):
        for k in far:
            send(block, block, ssem, rsem, at_gy(lax.rem(h + 2 * k, NG)))

    def hand_on(seven, eight, rsem, dsem, drsem):
        arrived(seven, rsem)
        send(eight, eight, dsem, drsem, at_gy(mate))

    with jax.named_scope("tokens"):
        for c in own_tok:
            c.wait()
        spread(xs.at[:, own8, :], xsem.at[0], xsem.at[1])
        hand_on(xs.at[:, pl.ds(0, 56), :], xs.at[:, core64, :], xsem.at[1], xsem.at[2], xsem.at[3])
        arrived(xs.at[:, pl.ds(0, 64), :], xsem.at[3])

    slots = {}

    def slot_of(tq):
        slots[tq] = slots.get(tq, -1) + 1
        return slots[tq]

    def enc(q, v):
        return encode4(v) if q < 2 else encode2(v)

    def dec(q, v):
        return decode4(v) if q < 2 else decode2(v)

    def long_way(q, t):
        return (q + t) % 2

    def chunk(t, q, d, k):
        return part[t, q, pl.ds(2 * zat(way(d, k)), 2)]

    def send_whole(t, q, val, d, hops, slot):
        tq = 3 * t + q
        i = slot_of(tq)
        sbuf[tq, i] = enc(q, val)
        send(sbuf.at[tq, i], rbuf.at[tq, d, slot], rss, rsr.at[tq, d, slot], column(way(d, hops)))

    def send_last(t, q, val, d, hops, slot):
        tq = 3 * t + q
        i = slot_of(tq)
        sbuf[tq, i] = enc(q, val)
        for other in (True, False):
            y = 1 - yh if other else yh
            dst = fin.at[tq, slot + d + (2 if other else 0)]
            send(sbuf.at[tq, i, y], dst, rss, fsr.at[tq], column(way(d, hops), other))

    def send_pair(t, q):
        tq = 3 * t + q
        pbuf[tq] = enc(q, part[t, q, 2 * z + 1 - yh])
        send(pbuf.at[tq], fin.at[tq, 4], pss, fsr.at[tq], column(0, True))

    def taken(t, q, d, slot):
        tq = 3 * t + q
        arrived(rbuf.at[tq, d, slot], rsr.at[tq, d, slot])
        return dec(q, rbuf[tq, d, slot])

    def total(t, q, n):
        tq = 3 * t + q
        arrived(fin.at[tq, pl.ds(0, n)], fsr.at[tq])
        val = part[t, q, 2 * z + yh]
        for i in range(n):
            val = val + dec(q, fin[tq, i])
        return val

    def up(t, q):
        for u in range(2):
            for n in range(0, FL, 256):
                m = min(256, FL - n)
                val = jnp.dot(xs[t], wup[2 * q + u, :, n : n + m], preferred_element_type=F32)
                part[t, q, :, u, :, n : n + m] = val.reshape(16, 8, m)
        d = long_way(q, t)
        send_whole(t, q, chunk(t, q, d, 4), d, 1, 0)
        send_whole(t, q, chunk(t, q, 1 - d, 3), 1 - d, 1, 1)
        send_pair(t, q)

    def ring(t, q, d, s):
        val = chunk(t, q, d, 4 - s) + taken(t, q, d, s - 1)
        if s < 3:
            send_whole(t, q, val, d, 1, s)
        else:
            send_last(t, q, val, d, 1, 0)

    def gather(v, t):
        own = ag.at[v, :, t, zown, :]
        for d in range(2):
            for other in (True, False):
                send(own, own, ags, agr.at[t, v, d], column(way(d, 2), other))
        for d in range(2):
            for other in (True, False):
                send(own, own, ags, agr.at[t, v, 2], column(way(d, 1), other))
        send(own, own, ags, agr.at[t, v, 2], column(0, True))

    def relay(v, t, d):
        arrived(ag.at[v, :, t, pl.ds(0, 16), :], agr.at[t, v, d])
        rows = ag.at[v, :, t, pl.ds(pl.multiple_of(16 * zat(way(d, -2)), 16), 16), :]
        if d == long_way(v, t):
            send(rows, rows, ags, agr.at[t, v, 2], column(way(d, 2)))
        send(rows, rows, ags, agr.at[t, v, 2], column(way(d, 1)))

    def gathered(v, t):
        arrived(ag.at[v, :, t, pl.ds(0, 88), :], agr.at[t, v, 2])

    def hidden(t):
        val = total(t, 0, 5)
        gate, upper = val[0], val[1]
        val = total(t, 1, 5)
        gate_dot, upper_dot = val[0], val[1]
        silu_val, first, second = silu_parts(gate)
        ag[0, 0, t, zown, :] = (silu_val * upper).astype(BF16)
        ag[0, 1, t, zown, :] = (first * gate_dot * upper + silu_val * upper_dot).astype(BF16)
        gather(0, t)
        for i, a in enumerate((gate, upper, gate_dot, upper_dot)):
            act[t, i] = a

    def out(t):
        gathered(0, t)
        for n in range(0, DL, 256):
            cols = slice(n, n + 256)
            val = jnp.dot(ag[0, 0, t], wdn[0, :, cols], preferred_element_type=F32)
            osum[t, :, :, 0, :, cols] = val.reshape(2, 8, 8, 256)
            val = jnp.dot(ag[0, 1, t], wdn[0, :, cols], preferred_element_type=F32)
            val = val + jnp.dot(ag[0, 0, t], wdn[1, :, cols], preferred_element_type=F32)
            osum[t, :, :, 1, :, cols] = val.reshape(2, 8, 8, 256)
        osend[t] = encode2(osum[t, 1 - core])
        send(osend.at[t], ocore.at[t], oss.at[0], osr.at[t], at_gy(mate))

    def out_send(t):
        arrived(ocore.at[t], osr.at[t])
        val = osum[t, core] + decode2(ocore[t])
        osum[t, core] = val
        oown[t] = encode2(val)
        for k in far:
            dst = lax.rem(mine + k, 8)
            send(oown.at[t, dst], orecv.at[t, k], oss.at[1], osr.at[2 + t], at_gy(2 * dst + core))

    def grads(t):
        arrived(orecv.at[t, pl.ds(1, 7)], osr.at[2 + t])
        val = osum[t, core, mine]
        for k in range(1, 8):
            val = val + decode2(orecv[t, k])
        target = tgv[8 * t : 8 * t + 8, :].astype(F32)
        gs[t, 0, own8, :] = ((val[0] - target) * scale).astype(BF16)
        gs[t, 1, own8, :] = (val[1] * scale).astype(BF16)
        spread(gs.at[t, :, own8, :], gss.at[0], gsr.at[t])

    def grads_on(t):
        hand_on(gs.at[t, :, pl.ds(0, 56), :], gs.at[t, :, core64, :], gsr.at[t], gss.at[1], gsr.at[2 + t])

    def back(t):
        arrived(gs.at[t, :, pl.ds(0, 64), :], gsr.at[2 + t])
        for n in range(0, FL, 256):
            m = min(256, FL - n)
            val = tail_dot(gs[t, 0], wdn[0, n : n + m, :])
            part[t, 2, :, 0, :, n : n + m] = val.reshape(16, 8, m)
            val = tail_dot(gs[t, 1], wdn[0, n : n + m, :]) + tail_dot(gs[t, 0], wdn[1, n : n + m, :])
            part[t, 2, :, 1, :, n : n + m] = val.reshape(16, 8, m)
        for d in range(2):
            send_whole(t, 2, chunk(t, 2, d, 3), d, 1, 0)
        d = long_way(2, t)
        send_whole(t, 2, chunk(t, 2, d, 4), d, 2, 1)
        for d in range(2):
            send_last(t, 2, chunk(t, 2, d, 1), d, 1, 0)
        send_pair(t, 2)

    def fold(t, d):
        val = chunk(t, 2, d, 2) + taken(t, 2, d, 0)
        if d == long_way(2, t):
            val = val + taken(t, 2, d, 1)
        send_last(t, 2, val, d, 2, 5)

    def inner(t):
        val = total(t, 2, 9)
        back_val, back_dot = val[0], val[1]
        gate, upper, gate_dot, upper_dot = act[t, 0], act[t, 1], act[t, 2], act[t, 3]
        silu_val, first, second = silu_parts(gate)
        ag[1, 0, t, zown, :] = (
            back_dot * upper * first + back_val * upper_dot * first + back_val * upper * second * gate_dot
        ).astype(BF16)
        ag[1, 1, t, zown, :] = (back_dot * silu_val + back_val * first * gate_dot).astype(BF16)
        gather(1, t)

    def down(n):
        g0 = gs[:, 0, :, n : n + 256].reshape(TOKENS, 256)
        g1 = gs[:, 1, :, n : n + 256].reshape(TOKENS, 256)
        hid = ag[0, 0].reshape(TOKENS, FL)
        hid_dot = ag[0, 1].reshape(TOKENS, FL)
        hd[:, n : n + 256] = (lead_dot(hid_dot, g0) + lead_dot(hid, g1)).astype(BF16)

    with jax.named_scope("up"):
        for t in range(2):
            for q in range(2):
                if t == 0:
                    local[2 * q].wait()
                    local[2 * q + 1].wait()
                up(t, q)
        xt[...] = xs[...].reshape(TOKENS, DL).T
        xt_copy = local_copy(xt, xt_out, 9)
    with jax.named_scope("ring"):
        for s in range(1, 4):
            for t in range(2):
                for q in range(2):
                    for d in range(2):
                        if s > (0 if d == long_way(q, t) else 1):
                            ring(t, q, d, s)
    for t in range(2):
        with jax.named_scope("hidden%d" % t):
            hidden(t)
    for t in range(2):
        with jax.named_scope("relay%d" % t):
            for d in range(2):
                relay(0, t, d)
    for c in local[4:]:
        c.wait()
    own_tgt.wait()
    for t in range(2):
        with jax.named_scope("out%d" % t):
            out(t)
        with jax.named_scope("outs%d" % t):
            out_send(t)
    for t in range(2):
        with jax.named_scope("grads%d" % t):
            grads(t)
    for t in range(2):
        with jax.named_scope("gradson%d" % t):
            grads_on(t)
        with jax.named_scope("back%d" % t):
            back(t)
    with jax.named_scope("down"):
        down(0)
        down(256)
        hd_copy = local_copy(hd, hd_out, 10)
    for t in range(2):
        with jax.named_scope("fold%d" % t):
            for d in range(2):
                fold(t, d)
    for t in range(2):
        with jax.named_scope("inner%d" % t):
            inner(t)
    for t in range(2):
        with jax.named_scope("relayb%d" % t):
            for d in range(2):
                relay(1, t, d)
    for t in range(2):
        with jax.named_scope("gathered%d" % t):
            gathered(1, t)
    with jax.named_scope("tail"):
        ag_copy = local_copy(ag.at[1], ag_out, 11)
        left(xs.at[:, pl.ds(0, 56), :], xsem.at[0])
        left(xs.at[:, pl.ds(0, 64), :], xsem.at[2])
        left(sbuf, rss)
        left(pbuf, pss)
        left(ag.at[:, :, :, pl.ds(0, 120), :], ags)
        left(osend, oss.at[0])
        left(oown.at[:, pl.ds(0, 7)], oss.at[1])
        left(gs.at[:, :, pl.ds(0, 56), :], gss.at[0])
        left(gs.at[:, :, pl.ds(0, 64), :], gss.at[1])
        xt_copy.wait()
        hd_copy.wait()
        ag_copy.wait()


def weights_kernel(xt, ag, hd, gate_out, up_out, down_out, buf, sem):
    rows = DL // 4
    down = pltpu.make_async_copy(hd, down_out, sem.at[8])
    down.start()
    copies = []
    for v, out in enumerate((gate_out, up_out)):
        for i in range(4):
            part = pl.ds(i * rows, rows)
            buf[v, part, :] = jnp.dot(xt[part, :], ag[v], preferred_element_type=F32).astype(BF16)
            copy = pltpu.make_async_copy(buf.at[v, part, :], out.at[part, :], sem.at[4 * v + i])
            copy.start()
            copies.append(copy)
    down.wait()
    for copy in copies:
        copy.wait()


def body(*args):
    hbm = pl.BlockSpec(memory_space=pltpu.HBM)
    vmem = pl.BlockSpec(memory_space=pltpu.VMEM)
    dma = pltpu.SemaphoreType.DMA
    args = [pltpu.with_memory_space_constraint(a, pltpu.HBM) for a in args]
    xt, ag, hd = pl.pallas_call(
        kernel,
        out_shape=(
            jax.ShapeDtypeStruct((DL, TOKENS), BF16),
            jax.ShapeDtypeStruct((2, 2, 128, FL), BF16),
            jax.ShapeDtypeStruct((FL, DL), BF16),
        ),
        in_specs=[hbm] * 8,
        out_specs=(pl.BlockSpec(memory_space=pl.ANY),) * 3,
        scratch_shapes=[
            pltpu.VMEM((2, 128, DL), BF16),
            pltpu.VMEM((DL, TOKENS), BF16),
            pltpu.VMEM((FL, DL), BF16),
            pltpu.VMEM((TOKENS // NG, DL), BF16),
            pltpu.VMEM((4, DL, FL), BF16),
            pltpu.VMEM((2, FL, DL), BF16),
            pltpu.VMEM((2, 3, 16, 2, 8, FL), F32),
            pltpu.VMEM((6, 7, 2, 2, 8, FL), BF16),
            pltpu.VMEM((6, 2, 3, 2, 2, 8, FL), BF16),
            pltpu.VMEM((6, 2, 8, FL), BF16),
            pltpu.VMEM((6, 9, 2, 8, FL), BF16),
            pltpu.VMEM((2, 4, 8, FL), F32),
            pltpu.VMEM((2, 2, 2, 128, FL), BF16),
            pltpu.VMEM((2, 2, 8, 2, 8, DL), F32),
            pltpu.VMEM((2, 8, 2, 8, DL), BF16),
            pltpu.VMEM((2, 8, 2, 8, DL), BF16),
            pltpu.VMEM((2, 8, 2, 8, DL), BF16),
            pltpu.VMEM((2, 8, 2, 8, DL), BF16),
            pltpu.VMEM((2, 2, 128, DL), BF16),
            dma((12,)),
            dma((4,)),
            dma, dma,
            dma((6, 2, 3)),
            dma((6,)),
            dma,
            dma((2, 2, 3)),
            dma((2,)), dma((4,)),
            dma((2,)), dma((4,)),
        ],
        compiler_params=pltpu.CompilerParams(
            collective_id=0, has_side_effects=True, vmem_limit_bytes=40 * 1024 * 1024
        ),
    )(*args)
    return pl.pallas_call(
        weights_kernel,
        out_shape=(
            jax.ShapeDtypeStruct((DL, FL), BF16),
            jax.ShapeDtypeStruct((DL, FL), BF16),
            jax.ShapeDtypeStruct((FL, DL), BF16),
        ),
        in_specs=[vmem] * 3,
        out_specs=(hbm,) * 3,
        scratch_shapes=[pltpu.VMEM((2, DL, FL), BF16), dma((9,))],
        compiler_params=pltpu.CompilerParams(vmem_limit_bytes=16 * 1024 * 1024),
    )(xt, ag.reshape(2, TOKENS, FL), hd)


def solution(mesh):
    in_specs = (
        P("gy", "gx"),
        P("gy", "gx"),
        P("gx", "gy"),
        P("gx", "gy"),
        P("gy", "gx"),
        P("gx", "gy"),
        P("gx", "gy"),
        P("gy", "gx"),
    )
    out_specs = (P("gx", "gy"), P("gx", "gy"), P("gy", "gx"))
    return jax.shard_map(body, mesh=mesh, in_specs=in_specs, out_specs=out_specs, check_vma=False)
```

time: 273 us -> 93.2 us (0.34)
  blocking collectives: 135 us -> 0 us
  waiting for transfers between devices: 96.7 us -> 0 us
  Pallas kernels: 0 us -> 91.7 us
  between operations: 14.2 us -> 0.64 us
  matrix products: 8.44 us -> 0 us
  starting transfers between devices: 8.19 us -> 0 us
  local copies, waits for them, and re-layouts: 5.49 us -> 0 us
  other arithmetic: 3.21 us -> 0 us
    all_gather x3 -> x0, blocking collectives: 101 us -> none  [sent_together(): filled, at, outs = (lax.all_gather(both, axis, axis=dim, tiled=True), 0, [])]
    pallas_call x0 -> x2, Pallas kernels: none -> 91.7 us  [the longest x1 90.1 us: body(): pl.pallas_call(kernel, out_shape=(jax.ShapeDtypeStruct((DL, TOKENS), BF16...]
    reduce_scatter x2 -> x0, waiting for transfers between devices: 73.2 us -> none  [reduced_to_own(): parts = lax.psum_scatter(parts, axes[k], scatter_dimension=0, tiled=True)]
    all_to_all x2 -> x0, blocking collectives: 33.5 us -> none  [the longest x1 20.6 us: sum_at_owner(): parts = lax.all_to_all(split_up(value, dim, length), axis, 0, 0, tiled=True)]
    all_to_all x1 -> x0, waiting for transfers between devices: 23.5 us -> none  [summed_on_arrival(): lax.all_to_all(parts, axis, split_axis=0, concat_axis=0, tiled=True)]
    dot_general x11 -> x0, matrix products: 8.44 us -> none  [the longest x4 4.41 us: matmul(): return jnp.dot(left, right, preferred_element_type=jnp.float32)]
    all_to_all x1 -> x0, starting transfers between devices: 8.11 us -> none  [summed_on_arrival(): lax.all_to_all(parts, axis, split_axis=0, concat_axis=0, tiled=True)]
  transfers between devices with their start and end apart: 3 -> 0, of which waited for: 3 -> 0; matrix products, arithmetic and copies ran while one was open for 1% -> 0% of each run, Pallas kernels for 0% -> 0%
where the time goes in v3:
time: 93.2 us; the launch traced here: 92.3 us
  Pallas kernels  91.7 us (98%)
    pallas_call x1, Pallas kernels, body(): pl.pallas_call(kernel, out_shape=(jax.ShapeDtypeStruct((DL, TOKENS), BF16...  90.1 us

profile of v3, /device:TPU:32, one launch (start us, length us, event | category | flops | bytes accessed | tf_op | source)
XLA Modules:
  0.0 92.3 jit_solution(3241971145409261539)
XLA Ops:
  0.6 90.1 %shard_map.103 = (bf16[512,256]{1,0:T(8,128)(2,1)S(1)}, bf16[2,2,128,896]{3,2,1,0:T(8,128)(2,1)S(1)}, bf16[896,512]{1,0:T(8,128)(2,1)S(1)}) custom-call(bf16[16,512]{1,0:T(8,128)(2,1)} %tok.1, bf16[16,512]{1,0:T(8,128)(2,1)} %tgt.1, bf16[512,896]{1,0:T(8,128)(2,1)} %wg.1, bf16[512,896]{1,0:T(8,128)(2,1)} %wu.1, bf16[896,512]{1,0:T(8,128)(2,1)} %wd.1, ...), custom_call_target="tpu_custom_call" | custom-call | tf_op jit(solution)/shard_map/pallas_call | solution.py:407
  90.7 1.6 %shard_map.104 = (bf16[512,896]{1,0:T(8,128)(2,1)}, bf16[512,896]{1,0:T(8,128)(2,1)}, bf16[896,512]{1,0:T(8,128)(2,1)}) custom-call(bf16[512,256]{1,0:T(8,128)(2,1)S(1)} %get-tuple-element.6.xt, bf16[2,256,896]{2,1,0:T(8,128)(2,1)S(1)} %bitcast.1, bf16[896,512]{1,0:T(8,128)(2,1)S(1)} %get-tuple-element.8.hd), custom_call_target="tpu_custom_call" | custom-call | tf_op jit(solution)/shard_map/pallas_call | solution.py:450

commit v4 on v3

--- a/solution.py
+++ b/solution.py
@@ -33,14 +33,16 @@
     return lax.dot_general(left, right, (((1,), (1,)), ((), ())), preferred_element_type=F32)
 
 
+TINY = 1e-36
+
+
 def encode2(v):
     return (v * jnp.abs(v)).astype(BF16)
 
 
 def decode2(c):
     v = c.astype(F32)
-    root = jnp.sqrt(jnp.abs(v))
-    return jnp.where(v < 0.0, -root, root)
+    return v * lax.rsqrt(jnp.maximum(jnp.abs(v), TINY))
 
 
 def encode4(v):
@@ -49,15 +51,27 @@
 
 def decode4(c):
     v = c.astype(F32)
-    root = jnp.sqrt(jnp.sqrt(jnp.abs(v)))
-    return jnp.where(v < 0.0, -root, root)
+    w = lax.rsqrt(jnp.maximum(jnp.abs(v), TINY))
+    return v * w * (w * lax.rsqrt(w))
+
+
+ORDER = (
+    ("up", 0, 1), ("cross0", 0), ("up", 0, 0), ("start", 0), ("up", 1, 1), ("cross0", 1), ("cross1", 0), ("up", 1, 0), ("start", 1), ("cross1", 1),
+    ("half", 0, 0, 0), ("half", 0, 1, 1), ("full", 0, 0, 1), ("half", 1, 0, 0), ("half", 1, 1, 1), ("full", 1, 0, 1), ("flat", 0), ("flat", 1),
+    ("half", 0, 0, 1), ("full", 0, 0, 2), ("full", 0, 1, 2), ("half", 1, 0, 1), ("full", 1, 0, 2), ("full", 1, 1, 2),
+    ("half", 0, 0, 2), ("half", 0, 1, 2), ("full", 0, 0, 3), ("full", 0, 1, 3), ("half", 1, 0, 2), ("half", 1, 1, 2), ("full", 1, 0, 3), ("full", 1, 1, 3),
+    ("half", 0, 0, 3), ("half", 0, 1, 3), ("half", 1, 0, 3), ("half", 1, 1, 3),
+    ("hidden", 0), ("hidden", 1), ("pass", 0), ("pass", 1), ("out", 0), ("outs", 0), ("out", 1), ("outs", 1),
+    ("grads", 0), ("grads", 1), ("on", 0), ("back", 0), ("on", 1), ("back", 1), ("down", 0), ("down", 256),
+    ("fold", 0), ("fold", 1), ("inner", 0), ("inner", 1), ("pass1", 0), ("pass1", 1),
+)
 
 
 def kernel(
     tok, tgt, wg, wu, wd, tg, tu, td,
     xt_out, ag_out, hd_out,
-    xs, xt, hd, tgv, wup, wdn, part, sbuf, rbuf, pbuf, fin, act, ag, osum, osend, ocore, oown, orecv, gs,
-    lsem, xsem, rss, pss, rsr, fsr, ags, agr, oss, osr, gss, gsr,
+    xs, xt, hd, tgv, wup, wdn, part, sbuf, rbuf, pbuf, fin, ysb, yrb, hsb, hrb, act, ag, osum, osend, ocore, oown, orecv, gs,
+    lsem, xsem, rss, pss, rsr, fsr, yss, ysr, hss, hsr, ags, agr, oss, osr, gss, gsr,
 ):
     scale = 1.0 / math.sqrt(TOKENS)
     g = lax.axis_index("gx")
@@ -150,16 +164,16 @@
         return (q + t) % 2
 
     def chunk(t, q, d, k):
-        return part[t, q, pl.ds(2 * zat(way(d, k)), 2)]
+        return part[t, q, zat(way(d, k))]
 
     def send_whole(t, q, val, d, hops, slot):
-        tq = 3 * t + q
+        tq = 2 * t + q // 2
         i = slot_of(tq)
         sbuf[tq, i] = enc(q, val)
         send(sbuf.at[tq, i], rbuf.at[tq, d, slot], rss, rsr.at[tq, d, slot], column(way(d, hops)))
 
     def send_last(t, q, val, d, hops, slot):
-        tq = 3 * t + q
+        tq = 2 * t + q // 2
         i = slot_of(tq)
         sbuf[tq, i] = enc(q, val)
         for other in (True, False):
@@ -168,19 +182,19 @@
             send(sbuf.at[tq, i, y], dst, rss, fsr.at[tq], column(way(d, hops), other))
 
     def send_pair(t, q):
-        tq = 3 * t + q
-        pbuf[tq] = enc(q, part[t, q, 2 * z + 1 - yh])
+        tq = 2 * t + q // 2
+        pbuf[tq] = enc(q, part[t, q, z, 1 - yh])
         send(pbuf.at[tq], fin.at[tq, 4], pss, fsr.at[tq], column(0, True))
 
     def taken(t, q, d, slot):
-        tq = 3 * t + q
+        tq = 2 * t + q // 2
         arrived(rbuf.at[tq, d, slot], rsr.at[tq, d, slot])
         return dec(q, rbuf[tq, d, slot])
 
     def total(t, q, n):
-        tq = 3 * t + q
+        tq = 2 * t + q // 2
         arrived(fin.at[tq, pl.ds(0, n)], fsr.at[tq])
-        val = part[t, q, 2 * z + yh]
+        val = part[t, q, z, yh]
         for i in range(n):
             val = val + dec(q, fin[tq, i])
         return val
@@ -190,11 +204,13 @@
             for n in range(0, FL, 256):
                 m = min(256, FL - n)
                 val = jnp.dot(xs[t], wup[2 * q + u, :, n : n + m], preferred_element_type=F32)
-                part[t, q, :, u, :, n : n + m] = val.reshape(16, 8, m)
-        d = long_way(q, t)
-        send_whole(t, q, chunk(t, q, d, 4), d, 1, 0)
-        send_whole(t, q, chunk(t, q, 1 - d, 3), 1 - d, 1, 1)
-        send_pair(t, q)
+                part[t, q, :, :, u, :, n : n + m] = val.reshape(8, 2, 8, m)
+
+    def ring_start(t):
+        d = long_way(0, t)
+        send_whole(t, 0, chunk(t, 0, d, 4), d, 1, 0)
+        send_whole(t, 0, chunk(t, 0, 1 - d, 3), 1 - d, 1, 1)
+        send_pair(t, 0)
 
     def ring(t, q, d, s):
         val = chunk(t, q, d, 4 - s) + taken(t, q, d, s - 1)
@@ -202,6 +218,35 @@
             send_whole(t, q, val, d, 1, s)
         else:
             send_last(t, q, val, d, 1, 0)
+
+    def cross(t, ks):
+        d = long_way(1, t)
+        for k in ks:
+            i = way(d, k) % NZ
+            ysb[t, i] = enc(0, part[t, 1, zat(i), 1 - yh])
+            send(ysb.at[t, i], yrb.at[t, i], yss, ysr.at[t, i], column(0, True))
+
+    def crossed(t, k):
+        i = k % NZ
+        arrived(yrb.at[t, i], ysr.at[t, i])
+        return part[t, 1, zat(i), yh] + dec(0, yrb[t, i])
+
+    def half_ring(t, d, s):
+        val = crossed(t, way(d, 4 - s))
+        first = 0 if d == long_way(1, t) else 1
+        if s > first:
+            arrived(hrb.at[t, d, s - 1], hsr.at[t, d, s - 1])
+            val = val + dec(0, hrb[t, d, s - 1])
+        i = slot_of(10 + t)
+        hsb[t, i] = enc(0, val)
+        send(hsb.at[t, i], hrb.at[t, d, s], hss, hsr.at[t, d, s], column(way(d, 1)))
+
+    def half_total(t):
+        val = crossed(t, 0)
+        for d in range(2):
+            arrived(hrb.at[t, d, 3], hsr.at[t, d, 3])
+            val = val + dec(0, hrb[t, d, 3])
+        return val
 
     def gather(v, t):
         own = ag.at[v, :, t, zown, :]
@@ -226,7 +271,7 @@
     def hidden(t):
         val = total(t, 0, 5)
         gate, upper = val[0], val[1]
-        val = total(t, 1, 5)
+        val = half_total(t)
         gate_dot, upper_dot = val[0], val[1]
         silu_val, first, second = silu_parts(gate)
         ag[0, 0, t, zown, :] = (silu_val * upper).astype(BF16)
@@ -274,9 +319,9 @@
         for n in range(0, FL, 256):
             m = min(256, FL - n)
             val = tail_dot(gs[t, 0], wdn[0, n : n + m, :])
-            part[t, 2, :, 0, :, n : n + m] = val.reshape(16, 8, m)
+            part[t, 2, :, :, 0, :, n : n + m] = val.reshape(8, 2, 8, m)
             val = tail_dot(gs[t, 1], wdn[0, n : n + m, :]) + tail_dot(gs[t, 0], wdn[1, n : n + m, :])
-            part[t, 2, :, 1, :, n : n + m] = val.reshape(16, 8, m)
+            part[t, 2, :, :, 1, :, n : n + m] = val.reshape(8, 2, 8, m)
         for d in range(2):
             send_whole(t, 2, chunk(t, 2, d, 3), d, 1, 0)
         d = long_way(2, t)
@@ -309,60 +354,57 @@
         hid_dot = ag[0, 1].reshape(TOKENS, FL)
         hd[:, n : n + 256] = (lead_dot(hid_dot, g0) + lead_dot(hid, g1)).astype(BF16)
 
-    with jax.named_scope("up"):
-        for t in range(2):
-            for q in range(2):
-                if t == 0:
-                    local[2 * q].wait()
-                    local[2 * q + 1].wait()
-                up(t, q)
-        xt[...] = xs[...].reshape(TOKENS, DL).T
-        xt_copy = local_copy(xt, xt_out, 9)
-    with jax.named_scope("ring"):
-        for s in range(1, 4):
-            for t in range(2):
-                for q in range(2):
-                    for d in range(2):
-                        if s > (0 if d == long_way(q, t) else 1):
-                            ring(t, q, d, s)
-    for t in range(2):
-        with jax.named_scope("hidden%d" % t):
-            hidden(t)
-    for t in range(2):
-        with jax.named_scope("relay%d" % t):
-            for d in range(2):
-                relay(0, t, d)
-    for c in local[4:]:
-        c.wait()
-    own_tgt.wait()
-    for t in range(2):
-        with jax.named_scope("out%d" % t):
-            out(t)
-        with jax.named_scope("outs%d" % t):
-            out_send(t)
-    for t in range(2):
-        with jax.named_scope("grads%d" % t):
-            grads(t)
-    for t in range(2):
-        with jax.named_scope("gradson%d" % t):
-            grads_on(t)
-        with jax.named_scope("back%d" % t):
-            back(t)
-    with jax.named_scope("down"):
-        down(0)
-        down(256)
-        hd_copy = local_copy(hd, hd_out, 10)
-    for t in range(2):
-        with jax.named_scope("fold%d" % t):
-            for d in range(2):
-                fold(t, d)
-    for t in range(2):
-        with jax.named_scope("inner%d" % t):
-            inner(t)
-    for t in range(2):
-        with jax.named_scope("relayb%d" % t):
-            for d in range(2):
-                relay(1, t, d)
+    def flat(t):
+        xt[:, 128 * t : 128 * t + 128] = xs[t].T
+
+    def both(f, *a):
+        for d in range(2):
+            f(*a, d)
+
+    def up_waited(t, q):
+        if t == 0:
+            local[2 * q].wait()
+            local[2 * q + 1].wait()
+        up(t, q)
+
+    def out_waited(t):
+        if t == 0:
+            for c in local[4:]:
+                c.wait()
+            own_tgt.wait()
+        out(t)
+
+    def half_way(t, short, s):
+        half_ring(t, (long_way(1, t) + short) % 2, s)
+
+    def full_way(t, short, s):
+        ring(t, 0, (long_way(0, t) + short) % 2, s)
+
+    steps = {
+        "up": up_waited,
+        "cross0": lambda t: cross(t, (4, -3, 3)),
+        "cross1": lambda t: cross(t, (2, -2, 1, -1, 0)),
+        "start": ring_start,
+        "half": half_way,
+        "full": full_way,
+        "hidden": hidden,
+        "pass": lambda t: both(relay, 0, t),
+        "out": out_waited,
+        "outs": out_send,
+        "grads": grads,
+        "on": grads_on,
+        "back": back,
+        "fold": lambda t: both(fold, t),
+        "inner": inner,
+        "pass1": lambda t: both(relay, 1, t),
+        "down": down,
+        "flat": flat,
+    }
+    for name, *a in ORDER:
+        with jax.named_scope(name + "_".join(str(i) for i in a)):
+            steps[name](*a)
+    xt_copy = local_copy(xt, xt_out, 9)
+    hd_copy = local_copy(hd, hd_out, 10)
     for t in range(2):
         with jax.named_scope("gathered%d" % t):
             gathered(1, t)
@@ -372,6 +414,8 @@
         left(xs.at[:, pl.ds(0, 64), :], xsem.at[2])
         left(sbuf, rss)
         left(pbuf, pss)
+        left(ysb, yss)
+        left(hsb, hss)
         left(ag.at[:, :, :, pl.ds(0, 120), :], ags)
         left(osend, oss.at[0])
         left(oown.at[:, pl.ds(0, 7)], oss.at[1])
@@ -420,11 +464,15 @@
             pltpu.VMEM((TOKENS // NG, DL), BF16),
             pltpu.VMEM((4, DL, FL), BF16),
             pltpu.VMEM((2, FL, DL), BF16),
-            pltpu.VMEM((2, 3, 16, 2, 8, FL), F32),
-            pltpu.VMEM((6, 7, 2, 2, 8, FL), BF16),
-            pltpu.VMEM((6, 2, 3, 2, 2, 8, FL), BF16),
-            pltpu.VMEM((6, 2, 8, FL), BF16),
-            pltpu.VMEM((6, 9, 2, 8, FL), BF16),
+            pltpu.VMEM((2, 3, 8, 2, 2, 8, FL), F32),
+            pltpu.VMEM((4, 7, 2, 2, 8, FL), BF16),
+            pltpu.VMEM((4, 2, 3, 2, 2, 8, FL), BF16),
+            pltpu.VMEM((4, 2, 8, FL), BF16),
+            pltpu.VMEM((4, 9, 2, 8, FL), BF16),
+            pltpu.VMEM((2, 8, 2, 8, FL), BF16),
+            pltpu.VMEM((2, 8, 2, 8, FL), BF16),
+            pltpu.VMEM((2, 7, 2, 8, FL), BF16),
+            pltpu.VMEM((2, 2, 4, 2, 8, FL), BF16),
             pltpu.VMEM((2, 4, 8, FL), F32),
             pltpu.VMEM((2, 2, 2, 128, FL), BF16),
             pltpu.VMEM((2, 2, 8, 2, 8, DL), F32),
@@ -436,8 +484,10 @@
             dma((12,)),
             dma((4,)),
             dma, dma,
-            dma((6, 2, 3)),
-            dma((6,)),
+            dma((4, 2, 3)),
+            dma((4,)),
+            dma, dma((2, 8)),
+            dma, dma((2, 2, 4)),
             dma,
             dma((2, 2, 3)),
             dma((2,)), dma((4,)),

time: 93.2 us -> 92.4 us (level)
  Pallas kernels: 91.7 us -> 90.5 us
    pallas_call x1, Pallas kernels: 90.1 us -> 88.8 us  [body(): pl.pallas_call(kernel, out_shape=(jax.ShapeDtypeStruct((DL, TOKENS), BF16...]
where the time goes in v4:
time: 92.4 us; the launch traced here: 91.1 us
  Pallas kernels  90.5 us (98%)
    pallas_call x1, Pallas kernels, body(): pl.pallas_call(kernel, out_shape=(jax.ShapeDtypeStruct((DL, TOKENS), BF16...  88.8 us

profile of v4, /device:TPU:32, one launch (start us, length us, event | category | flops | bytes accessed | tf_op | source)
XLA Modules:
  0.0 91.1 jit_solution(1501454322549014833)
XLA Ops:
  0.6 88.8 %shard_map.103 = (bf16[512,256]{1,0:T(8,128)(2,1)S(1)}, bf16[2,2,128,896]{3,2,1,0:T(8,128)(2,1)S(1)}, bf16[896,512]{1,0:T(8,128)(2,1)S(1)}) custom-call(bf16[16,512]{1,0:T(8,128)(2,1)} %tok.1, bf16[16,512]{1,0:T(8,128)(2,1)} %tgt.1, bf16[512,896]{1,0:T(8,128)(2,1)} %wg.1, bf16[512,896]{1,0:T(8,128)(2,1)} %wu.1, bf16[896,512]{1,0:T(8,128)(2,1)} %wd.1, ...), custom_call_target="tpu_custom_call" | custom-call | tf_op jit(solution)/shard_map/pallas_call | solution.py:451
  89.5 1.6 %shard_map.104 = (bf16[512,896]{1,0:T(8,128)(2,1)}, bf16[512,896]{1,0:T(8,128)(2,1)}, bf16[896,512]{1,0:T(8,128)(2,1)}) custom-call(bf16[512,256]{1,0:T(8,128)(2,1)S(1)} %get-tuple-element.6.xt, bf16[2,256,896]{2,1,0:T(8,128)(2,1)S(1)} %bitcast.1, bf16[896,512]{1,0:T(8,128)(2,1)S(1)} %get-tuple-element.8.hd), custom_call_target="tpu_custom_call" | custom-call | tf_op jit(solution)/shard_map/pallas_call | solution.py:500

commit v5 on v4

--- a/solution.py
+++ b/solution.py
@@ -57,21 +57,22 @@
 
 ORDER = (
     ("up", 0, 1), ("cross0", 0), ("up", 0, 0), ("start", 0), ("up", 1, 1), ("cross0", 1), ("cross1", 0), ("up", 1, 0), ("start", 1), ("cross1", 1),
-    ("half", 0, 0, 0), ("half", 0, 1, 1), ("full", 0, 0, 1), ("half", 1, 0, 0), ("half", 1, 1, 1), ("full", 1, 0, 1), ("flat", 0), ("flat", 1),
-    ("half", 0, 0, 1), ("full", 0, 0, 2), ("full", 0, 1, 2), ("half", 1, 0, 1), ("full", 1, 0, 2), ("full", 1, 1, 2),
-    ("half", 0, 0, 2), ("half", 0, 1, 2), ("full", 0, 0, 3), ("full", 0, 1, 3), ("half", 1, 0, 2), ("half", 1, 1, 2), ("full", 1, 0, 3), ("full", 1, 1, 3),
-    ("half", 0, 0, 3), ("half", 0, 1, 3), ("half", 1, 0, 3), ("half", 1, 1, 3),
-    ("hidden", 0), ("hidden", 1), ("pass", 0), ("pass", 1), ("out", 0), ("outs", 0), ("out", 1), ("outs", 1),
-    ("grads", 0), ("grads", 1), ("on", 0), ("back", 0), ("on", 1), ("back", 1), ("down", 0), ("down", 256),
-    ("fold", 0), ("fold", 1), ("inner", 0), ("inner", 1), ("pass1", 0), ("pass1", 1),
+    ("full", 0, 0, 1), ("half", 0, 0, 0), ("half", 0, 1, 1), ("full", 1, 0, 1), ("half", 1, 0, 0), ("half", 1, 1, 1), ("full", 0, 0, 2),
+    ("full", 0, 1, 2), ("half", 0, 0, 1), ("full", 1, 0, 2), ("full", 1, 1, 2), ("half", 1, 0, 1), ("full", 0, 0, 3), ("full", 0, 1, 3),
+    ("half", 0, 0, 2), ("half", 0, 1, 2), ("full", 1, 0, 3), ("full", 1, 1, 3), ("half", 1, 0, 2), ("half", 1, 1, 2), ("flat", 0), ("flat", 1),
+    ("hidden", 0), ("half", 0, 0, 3), ("half", 0, 1, 3), ("hidden", 1), ("half", 1, 0, 3), ("half", 1, 1, 3), ("hiddent", 0), ("hiddent", 1),
+    ("pass", 0), ("pass", 1), ("passt", 0), ("passt", 1), ("out", 0, 0), ("out", 1, 0), ("outs", 0, 0), ("outs", 1, 0), ("out", 0, 1), ("out", 1, 1),
+    ("outs", 0, 1), ("outs", 1, 1), ("grads", 0, 0), ("grads", 1, 0), ("grads", 0, 1), ("grads", 1, 1), ("back", 0, 0), ("back", 1, 0),
+    ("back", 0, 1), ("back", 1, 1), ("down", 0), ("down", 256), ("fold", 0, 0), ("fold", 1, 0), ("fold", 0, 1), ("fold", 1, 1), ("inner", 0),
+    ("inner", 1), ("pass1", 0), ("pass1", 1),
 )
 
 
 def kernel(
     tok, tgt, wg, wu, wd, tg, tu, td,
     xt_out, ag_out, hd_out,
-    xs, xt, hd, tgv, wup, wdn, part, sbuf, rbuf, pbuf, fin, ysb, yrb, hsb, hrb, act, ag, osum, osend, ocore, oown, orecv, gs,
-    lsem, xsem, rss, pss, rsr, fsr, yss, ysr, hss, hsr, ags, agr, oss, osr, gss, gsr,
+    xs, xt, hd, tgv, wup, wdn, part, sbuf, rbuf, pbuf, fin, ysb, yrb, hsb, hrb, bsb, brb, bpb, bfin, act, ag, osum, osend, ocore, oown, orecv, gs,
+    lsem, xsem, rss, pss, rsr, fsr, yss, ysr, hss, hsr, bsb_sem, brb_sem, bpb_sem, bfin_sem, ags, agr, oss, osr, gss, gsr,
 ):
     scale = 1.0 / math.sqrt(TOKENS)
     g = lax.axis_index("gx")
@@ -126,27 +127,20 @@
     with jax.named_scope("barrier"):
         barrier = pltpu.get_barrier_semaphore()
         near = [column(k, o) for k in (1, -1, 2, -2) for o in (False, True)] + [column(0, True)]
-        near += [at_gy(lax.rem(h + 2 * k, NG)) for k in range(1, 8)] + [at_gy(mate)]
+        near += [at_gy(lax.rem(h + k, NG)) for k in range(1, NG)]
         for where in near:
             pl.semaphore_signal(barrier, inc=1, device_id=where, device_id_type=MESH)
         pl.semaphore_wait(barrier, len(near))
 
     far = (4, 5, 3, 6, 2, 7, 1)
-
-    def spread(block, ssem, rsem):
-        for k in far:
-            send(block, block, ssem, rsem, at_gy(lax.rem(h + 2 * k, NG)))
-
-    def hand_on(seven, eight, rsem, dsem, drsem):
-        arrived(seven, rsem)
-        send(eight, eight, dsem, drsem, at_gy(mate))
+    all_far = (8, 10, 6, 9, 7, 11, 5, 12, 4, 14, 2, 13, 3, 15, 1)
 
     with jax.named_scope("tokens"):
         for c in own_tok:
             c.wait()
-        spread(xs.at[:, own8, :], xsem.at[0], xsem.at[1])
-        hand_on(xs.at[:, pl.ds(0, 56), :], xs.at[:, core64, :], xsem.at[1], xsem.at[2], xsem.at[3])
-        arrived(xs.at[:, pl.ds(0, 64), :], xsem.at[3])
+        for k in all_far:
+            send(xs.at[:, own8, :], xs.at[:, own8, :], xsem.at[0], xsem.at[1], at_gy(lax.rem(h + k, NG)))
+        arrived(xs.at[:, pl.ds(0, 120), :], xsem.at[1])
 
     slots = {}
 
@@ -167,13 +161,13 @@
         return part[t, q, zat(way(d, k))]
 
     def send_whole(t, q, val, d, hops, slot):
-        tq = 2 * t + q // 2
+        tq = t
         i = slot_of(tq)
         sbuf[tq, i] = enc(q, val)
         send(sbuf.at[tq, i], rbuf.at[tq, d, slot], rss, rsr.at[tq, d, slot], column(way(d, hops)))
 
     def send_last(t, q, val, d, hops, slot):
-        tq = 2 * t + q // 2
+        tq = t
         i = slot_of(tq)
         sbuf[tq, i] = enc(q, val)
         for other in (True, False):
@@ -182,17 +176,17 @@
             send(sbuf.at[tq, i, y], dst, rss, fsr.at[tq], column(way(d, hops), other))
 
     def send_pair(t, q):
-        tq = 2 * t + q // 2
+        tq = t
         pbuf[tq] = enc(q, part[t, q, z, 1 - yh])
         send(pbuf.at[tq], fin.at[tq, 4], pss, fsr.at[tq], column(0, True))
 
     def taken(t, q, d, slot):
-        tq = 2 * t + q // 2
+        tq = t
         arrived(rbuf.at[tq, d, slot], rsr.at[tq, d, slot])
         return dec(q, rbuf[tq, d, slot])
 
     def total(t, q, n):
-        tq = 2 * t + q // 2
+        tq = t
         arrived(fin.at[tq, pl.ds(0, n)], fsr.at[tq])
         val = part[t, q, z, yh]
         for i in range(n):
@@ -248,104 +242,127 @@
             val = val + dec(0, hrb[t, d, 3])
         return val
 
-    def gather(v, t):
-        own = ag.at[v, :, t, zown, :]
-        for d in range(2):
-            for other in (True, False):
-                send(own, own, ags, agr.at[t, v, d], column(way(d, 2), other))
-        for d in range(2):
-            for other in (True, False):
-                send(own, own, ags, agr.at[t, v, 2], column(way(d, 1), other))
-        send(own, own, ags, agr.at[t, v, 2], column(0, True))
-
-    def relay(v, t, d):
-        arrived(ag.at[v, :, t, pl.ds(0, 16), :], agr.at[t, v, d])
-        rows = ag.at[v, :, t, pl.ds(pl.multiple_of(16 * zat(way(d, -2)), 16), 16), :]
-        if d == long_way(v, t):
-            send(rows, rows, ags, agr.at[t, v, 2], column(way(d, 2)))
-        send(rows, rows, ags, agr.at[t, v, 2], column(way(d, 1)))
-
-    def gathered(v, t):
-        arrived(ag.at[v, :, t, pl.ds(0, 88), :], agr.at[t, v, 2])
-
-    def hidden(t):
+    def group(e, t, rows):
+        return ag.at[e // 2, pl.ds(0, 2) if e == 2 else pl.ds(e, 1), t, rows, :]
+
+    def gather(e, t):
+        own = group(e, t, zown)
+        for k, slot in ((2, 0), (1, 2)):
+            for d in range(2):
+                for other in (True, False):
+                    send(own, own, ags, agr.at[t, e, d if k == 2 else 2], column(way(d, k), other))
+        send(own, own, ags, agr.at[t, e, 2], column(0, True))
+
+    def relay(e, t, d):
+        arrived(group(e, t, pl.ds(0, 16)), agr.at[t, e, d])
+        rows = group(e, t, pl.ds(pl.multiple_of(16 * zat(way(d, -2)), 16), 16))
+        if d == long_way(e, t):
+            send(rows, rows, ags, agr.at[t, e, 2], column(way(d, 2)))
+        send(rows, rows, ags, agr.at[t, e, 2], column(way(d, 1)))
+
+    def gathered(e, t):
+        arrived(group(e, t, pl.ds(0, 88)), agr.at[t, e, 2])
+
+    def hidden_value(t):
         val = total(t, 0, 5)
-        gate, upper = val[0], val[1]
+        act[t, 0] = val[0]
+        act[t, 1] = val[1]
+        ag[0, 0, t, zown, :] = (silu_parts(val[0])[0] * val[1]).astype(BF16)
+        gather(0, t)
+
+    def hidden_tangent(t):
         val = half_total(t)
-        gate_dot, upper_dot = val[0], val[1]
+        gate, upper, gate_dot, upper_dot = act[t, 0], act[t, 1], val[0], val[1]
         silu_val, first, second = silu_parts(gate)
-        ag[0, 0, t, zown, :] = (silu_val * upper).astype(BF16)
         ag[0, 1, t, zown, :] = (first * gate_dot * upper + silu_val * upper_dot).astype(BF16)
-        gather(0, t)
-        for i, a in enumerate((gate, upper, gate_dot, upper_dot)):
-            act[t, i] = a
-
-    def out(t):
-        gathered(0, t)
+        gather(1, t)
+        act[t, 2] = gate_dot
+        act[t, 3] = upper_dot
+
+    def out(t, w):
+        gathered(w, t)
         for n in range(0, DL, 256):
             cols = slice(n, n + 256)
-            val = jnp.dot(ag[0, 0, t], wdn[0, :, cols], preferred_element_type=F32)
-            osum[t, :, :, 0, :, cols] = val.reshape(2, 8, 8, 256)
-            val = jnp.dot(ag[0, 1, t], wdn[0, :, cols], preferred_element_type=F32)
-            val = val + jnp.dot(ag[0, 0, t], wdn[1, :, cols], preferred_element_type=F32)
-            osum[t, :, :, 1, :, cols] = val.reshape(2, 8, 8, 256)
-        osend[t] = encode2(osum[t, 1 - core])
-        send(osend.at[t], ocore.at[t], oss.at[0], osr.at[t], at_gy(mate))
-
-    def out_send(t):
-        arrived(ocore.at[t], osr.at[t])
-        val = osum[t, core] + decode2(ocore[t])
-        osum[t, core] = val
-        oown[t] = encode2(val)
+            val = jnp.dot(ag[0, w, t], wdn[0, :, cols], preferred_element_type=F32)
+            if w == 1:
+                val = val + jnp.dot(ag[0, 0, t], wdn[1, :, cols], preferred_element_type=F32)
+            osum[t, w, :, :, :, cols] = val.reshape(2, 8, 8, 256)
+        osend[t, w] = encode2(osum[t, w, 1 - core])
+        send(osend.at[t, w], ocore.at[t, w], oss.at[0], osr.at[0, t, w], at_gy(mate))
+
+    def out_send(t, w):
+        arrived(ocore.at[t, w], osr.at[0, t, w])
+        val = osum[t, w, core] + decode2(ocore[t, w])
+        osum[t, w, core] = val
+        oown[t, w] = encode2(val)
         for k in far:
             dst = lax.rem(mine + k, 8)
-            send(oown.at[t, dst], orecv.at[t, k], oss.at[1], osr.at[2 + t], at_gy(2 * dst + core))
-
-    def grads(t):
-        arrived(orecv.at[t, pl.ds(1, 7)], osr.at[2 + t])
-        val = osum[t, core, mine]
+            send(oown.at[t, w, dst], orecv.at[t, w, k], oss.at[1], osr.at[1, t, w], at_gy(2 * dst + core))
+
+    def grads(t, w):
+        arrived(orecv.at[t, w, pl.ds(1, 7)], osr.at[1, t, w])
+        val = osum[t, w, core, mine]
         for k in range(1, 8):
-            val = val + decode2(orecv[t, k])
-        target = tgv[8 * t : 8 * t + 8, :].astype(F32)
-        gs[t, 0, own8, :] = ((val[0] - target) * scale).astype(BF16)
-        gs[t, 1, own8, :] = (val[1] * scale).astype(BF16)
-        spread(gs.at[t, :, own8, :], gss.at[0], gsr.at[t])
-
-    def grads_on(t):
-        hand_on(gs.at[t, :, pl.ds(0, 56), :], gs.at[t, :, core64, :], gsr.at[t], gss.at[1], gsr.at[2 + t])
-
-    def back(t):
-        arrived(gs.at[t, :, pl.ds(0, 64), :], gsr.at[2 + t])
+            val = val + decode2(orecv[t, w, k])
+        if w == 0:
+            val = val - tgv[8 * t : 8 * t + 8, :].astype(F32)
+        gs[t, w, own8, :] = (val * scale).astype(BF16)
+        own = gs.at[t, w, own8, :]
+        for k in all_far:
+            send(own, own, gss, gsr.at[t, w], at_gy(lax.rem(h + k, NG)))
+
+    def back(t, u):
+        arrived(gs.at[t, u, pl.ds(0, 120), :], gsr.at[t, u])
         for n in range(0, FL, 256):
             m = min(256, FL - n)
-            val = tail_dot(gs[t, 0], wdn[0, n : n + m, :])
-            part[t, 2, :, :, 0, :, n : n + m] = val.reshape(8, 2, 8, m)
-            val = tail_dot(gs[t, 1], wdn[0, n : n + m, :]) + tail_dot(gs[t, 0], wdn[1, n : n + m, :])
-            part[t, 2, :, :, 1, :, n : n + m] = val.reshape(8, 2, 8, m)
+            val = tail_dot(gs[t, u], wdn[0, n : n + m, :])
+            if u == 1:
+                val = val + tail_dot(gs[t, 0], wdn[1, n : n + m, :])
+            part[t, 2, :, :, u, :, n : n + m] = val.reshape(8, 2, 8, m)
         for d in range(2):
-            send_whole(t, 2, chunk(t, 2, d, 3), d, 1, 0)
-        d = long_way(2, t)
-        send_whole(t, 2, chunk(t, 2, d, 4), d, 2, 1)
+            back_far(t, u, d, 3, 1, 0)
+        back_far(t, u, (t + u) % 2, 4, 2, 1)
         for d in range(2):
-            send_last(t, 2, chunk(t, 2, d, 1), d, 1, 0)
-        send_pair(t, 2)
-
-    def fold(t, d):
-        val = chunk(t, 2, d, 2) + taken(t, 2, d, 0)
-        if d == long_way(2, t):
-            val = val + taken(t, 2, d, 1)
-        send_last(t, 2, val, d, 2, 5)
+            back_last(t, u, d, 1, part[t, 2, zat(way(d, 1)), :, u], 0)
+        bpb[t, u] = encode2(part[t, 2, z, 1 - yh, u])
+        send(bpb.at[t, u], bfin.at[t, u, 4], bpb_sem, bfin_sem.at[t, u], column(0, True))
+
+    def back_far(t, u, d, k, hops, slot):
+        i = slot_of((t, u))
+        bsb[t, u, i] = encode2(part[t, 2, zat(way(d, k)), :, u])
+        send(bsb.at[t, u, i], brb.at[t, u, d, slot], bsb_sem, brb_sem.at[t, u, d, slot], column(way(d, hops)))
+
+    def back_last(t, u, d, k, val, slot):
+        i = slot_of((t, u))
+        bsb[t, u, i] = encode2(val)
+        for other in (True, False):
+            y = 1 - yh if other else yh
+            dst = bfin.at[t, u, slot + d + (2 if other else 0)]
+            send(bsb.at[t, u, i, y], dst, bsb_sem, bfin_sem.at[t, u], column(way(d, k), other))
+
+    def fold(t, u, d):
+        val = part[t, 2, zat(way(d, 2)), :, u]
+        for slot in range(2 if d == (t + u) % 2 else 1):
+            arrived(brb.at[t, u, d, slot], brb_sem.at[t, u, d, slot])
+            val = val + decode2(brb[t, u, d, slot])
+        back_last(t, u, d, 2, val, 5)
+
+    def summed(t, u):
+        arrived(bfin.at[t, u], bfin_sem.at[t, u])
+        val = part[t, 2, z, yh, u]
+        for i in range(9):
+            val = val + decode2(bfin[t, u, i])
+        return val
 
     def inner(t):
-        val = total(t, 2, 9)
-        back_val, back_dot = val[0], val[1]
+        back_val, back_dot = summed(t, 0), summed(t, 1)
         gate, upper, gate_dot, upper_dot = act[t, 0], act[t, 1], act[t, 2], act[t, 3]
         silu_val, first, second = silu_parts(gate)
         ag[1, 0, t, zown, :] = (
             back_dot * upper * first + back_val * upper_dot * first + back_val * upper * second * gate_dot
         ).astype(BF16)
         ag[1, 1, t, zown, :] = (back_dot * silu_val + back_val * first * gate_dot).astype(BF16)
-        gather(1, t)
+        gather(2, t)
 
     def down(n):
         g0 = gs[:, 0, :, n : n + 256].reshape(TOKENS, 256)
@@ -367,12 +384,12 @@
             local[2 * q + 1].wait()
         up(t, q)
 
-    def out_waited(t):
+    def out_waited(t, w):
         if t == 0:
-            for c in local[4:]:
-                c.wait()
+            local[4 + w].wait()
+        if t == 0 and w == 0:
             own_tgt.wait()
-        out(t)
+        out(t, w)
 
     def half_way(t, short, s):
         half_ring(t, (long_way(1, t) + short) % 2, s)
@@ -387,16 +404,17 @@
         "start": ring_start,
         "half": half_way,
         "full": full_way,
-        "hidden": hidden,
+        "hidden": hidden_value,
+        "hiddent": hidden_tangent,
         "pass": lambda t: both(relay, 0, t),
+        "passt": lambda t: both(relay, 1, t),
         "out": out_waited,
         "outs": out_send,
         "grads": grads,
-        "on": grads_on,
         "back": back,
-        "fold": lambda t: both(fold, t),
+        "fold": lambda t, u: both(fold, t, u),
         "inner": inner,
-        "pass1": lambda t: both(relay, 1, t),
+        "pass1": lambda t: both(relay, 2, t),
         "down": down,
         "flat": flat,
     }
@@ -407,20 +425,20 @@
     hd_copy = local_copy(hd, hd_out, 10)
     for t in range(2):
         with jax.named_scope("gathered%d" % t):
-            gathered(1, t)
+            gathered(2, t)
     with jax.named_scope("tail"):
         ag_copy = local_copy(ag.at[1], ag_out, 11)
-        left(xs.at[:, pl.ds(0, 56), :], xsem.at[0])
-        left(xs.at[:, pl.ds(0, 64), :], xsem.at[2])
+        left(xs.at[:, pl.ds(0, 120), :], xsem.at[0])
         left(sbuf, rss)
         left(pbuf, pss)
         left(ysb, yss)
         left(hsb, hss)
+        left(bsb, bsb_sem)
+        left(bpb, bpb_sem)
         left(ag.at[:, :, :, pl.ds(0, 120), :], ags)
         left(osend, oss.at[0])
-        left(oown.at[:, pl.ds(0, 7)], oss.at[1])
-        left(gs.at[:, :, pl.ds(0, 56), :], gss.at[0])
-        left(gs.at[:, :, pl.ds(0, 64), :], gss.at[1])
+        left(oown.at[:, :, pl.ds(0, 7)], oss.at[1])
+        left(gs.at[:, :, pl.ds(0, 120), :], gss)
         xt_copy.wait()
         hd_copy.wait()
         ag_copy.wait()
@@ -465,33 +483,38 @@
             pltpu.VMEM((4, DL, FL), BF16),
             pltpu.VMEM((2, FL, DL), BF16),
             pltpu.VMEM((2, 3, 8, 2, 2, 8, FL), F32),
-            pltpu.VMEM((4, 7, 2, 2, 8, FL), BF16),
-            pltpu.VMEM((4, 2, 3, 2, 2, 8, FL), BF16),
-            pltpu.VMEM((4, 2, 8, FL), BF16),
-            pltpu.VMEM((4, 9, 2, 8, FL), BF16),
+            pltpu.VMEM((2, 7, 2, 2, 8, FL), BF16),
+            pltpu.VMEM((2, 2, 3, 2, 2, 8, FL), BF16),
+            pltpu.VMEM((2, 2, 8, FL), BF16),
+            pltpu.VMEM((2, 5, 2, 8, FL), BF16),
             pltpu.VMEM((2, 8, 2, 8, FL), BF16),
             pltpu.VMEM((2, 8, 2, 8, FL), BF16),
             pltpu.VMEM((2, 7, 2, 8, FL), BF16),
             pltpu.VMEM((2, 2, 4, 2, 8, FL), BF16),
+            pltpu.VMEM((2, 2, 7, 2, 8, FL), BF16),
+            pltpu.VMEM((2, 2, 2, 2, 2, 8, FL), BF16),
+            pltpu.VMEM((2, 2, 8, FL), BF16),
+            pltpu.VMEM((2, 2, 9, 8, FL), BF16),
             pltpu.VMEM((2, 4, 8, FL), F32),
             pltpu.VMEM((2, 2, 2, 128, FL), BF16),
-            pltpu.VMEM((2, 2, 8, 2, 8, DL), F32),
-            pltpu.VMEM((2, 8, 2, 8, DL), BF16),
-            pltpu.VMEM((2, 8, 2, 8, DL), BF16),
-            pltpu.VMEM((2, 8, 2, 8, DL), BF16),
-            pltpu.VMEM((2, 8, 2, 8, DL), BF16),
+            pltpu.VMEM((2, 2, 2, 8, 8, DL), F32),
+            pltpu.VMEM((2, 2, 8, 8, DL), BF16),
+            pltpu.VMEM((2, 2, 8, 8, DL), BF16),
+            pltpu.VMEM((2, 2, 8, 8, DL), BF16),
+            pltpu.VMEM((2, 2, 8, 8, DL), BF16),
             pltpu.VMEM((2, 2, 128, DL), BF16),
             dma((12,)),
             dma((4,)),
             dma, dma,
-            dma((4, 2, 3)),
-            dma((4,)),
+            dma((2, 2, 3)),
+            dma((2,)),
             dma, dma((2, 8)),
             dma, dma((2, 2, 4)),
+            dma, dma((2, 2, 2, 2)), dma, dma((2, 2)),
             dma,
-            dma((2, 2, 3)),
-            dma((2,)), dma((4,)),
-            dma((2,)), dma((4,)),
+            dma((2, 3, 3)),
+            dma((2,)), dma((2, 2, 2)),
+            dma, dma((2, 2)),
         ],
         compiler_params=pltpu.CompilerParams(
             collective_id=0, has_side_effects=True, vmem_limit_bytes=40 * 1024 * 1024

time: 92.4 us -> 88.4 us (0.957); the launches traced: 91.1 us -> 88.2 us
  Pallas kernels: 90.5 us -> 87.6 us
    pallas_call x1, Pallas kernels: 88.8 us -> 85.9 us  [body(): pl.pallas_call(kernel, out_shape=(jax.ShapeDtypeStruct((DL, TOKENS), BF16...]
where the time goes in v5:
time: 88.4 us; the launch traced here: 88.2 us
  Pallas kernels  87.6 us (99%)
    pallas_call x1, Pallas kernels, body(): pl.pallas_call(kernel, out_shape=(jax.ShapeDtypeStruct((DL, TOKENS), BF16...  85.9 us

profile of v5, /device:TPU:32, one launch (start us, length us, event | category | flops | bytes accessed | tf_op | source)
XLA Modules:
  0.0 88.2 jit_solution(18136781789996903488)
XLA Ops:
  0.6 85.9 %shard_map.103 = (bf16[512,256]{1,0:T(8,128)(2,1)S(1)}, bf16[2,2,128,896]{3,2,1,0:T(8,128)(2,1)S(1)}, bf16[896,512]{1,0:T(8,128)(2,1)S(1)}) custom-call(bf16[16,512]{1,0:T(8,128)(2,1)} %tok.1, bf16[16,512]{1,0:T(8,128)(2,1)} %tgt.1, bf16[512,896]{1,0:T(8,128)(2,1)} %wg.1, bf16[512,896]{1,0:T(8,128)(2,1)} %wu.1, bf16[896,512]{1,0:T(8,128)(2,1)} %wd.1, ...), custom_call_target="tpu_custom_call" | custom-call | tf_op jit(solution)/shard_map/pallas_call | solution.py:469
  86.6 1.6 %shard_map.104 = (bf16[512,896]{1,0:T(8,128)(2,1)}, bf16[512,896]{1,0:T(8,128)(2,1)}, bf16[896,512]{1,0:T(8,128)(2,1)}) custom-call(bf16[512,256]{1,0:T(8,128)(2,1)S(1)} %get-tuple-element.6.xt, bf16[2,256,896]{2,1,0:T(8,128)(2,1)S(1)} %bitcast.1, bf16[896,512]{1,0:T(8,128)(2,1)S(1)} %get-tuple-element.8.hd), custom_call_target="tpu_custom_call" | custom-call | tf_op jit(solution)/shard_map/pallas_call | solution.py:523

commit v6 on v5

--- a/solution.py
+++ b/solution.py
@@ -213,16 +213,24 @@
         else:
             send_last(t, q, val, d, 1, 0)
 
+    waited = set()
+
+    def cross_group(i):
+        return {4: 0, 3: 0, 5: 0, 2: 1, 6: 1}.get(i, 2)
+
     def cross(t, ks):
         d = long_way(1, t)
         for k in ks:
             i = way(d, k) % NZ
             ysb[t, i] = enc(0, part[t, 1, zat(i), 1 - yh])
-            send(ysb.at[t, i], yrb.at[t, i], yss, ysr.at[t, i], column(0, True))
+            send(ysb.at[t, i], yrb.at[t, i], yss, ysr.at[t, cross_group(i)], column(0, True))
 
     def crossed(t, k):
         i = k % NZ
-        arrived(yrb.at[t, i], ysr.at[t, i])
+        e = cross_group(i)
+        if (t, e) not in waited:
+            waited.add((t, e))
+            arrived(yrb.at[t, pl.ds(0, 2 if e == 1 else 3)], ysr.at[t, e])
         return part[t, 1, zat(i), yh] + dec(0, yrb[t, i])
 
     def half_ring(t, d, s):
@@ -330,7 +338,7 @@
     def back_far(t, u, d, k, hops, slot):
         i = slot_of((t, u))
         bsb[t, u, i] = encode2(part[t, 2, zat(way(d, k)), :, u])
-        send(bsb.at[t, u, i], brb.at[t, u, d, slot], bsb_sem, brb_sem.at[t, u, d, slot], column(way(d, hops)))
+        send(bsb.at[t, u, i], brb.at[t, u, d, slot], bsb_sem, brb_sem.at[t, u, 2 if slot else d], column(way(d, hops)))
 
     def back_last(t, u, d, k, val, slot):
         i = slot_of((t, u))
@@ -343,7 +351,7 @@
     def fold(t, u, d):
         val = part[t, 2, zat(way(d, 2)), :, u]
         for slot in range(2 if d == (t + u) % 2 else 1):
-            arrived(brb.at[t, u, d, slot], brb_sem.at[t, u, d, slot])
+            arrived(brb.at[t, u, d, slot], brb_sem.at[t, u, 2 if slot else d])
             val = val + decode2(brb[t, u, d, slot])
         back_last(t, u, d, 2, val, 5)
 
@@ -421,13 +429,14 @@
     for name, *a in ORDER:
         with jax.named_scope(name + "_".join(str(i) for i in a)):
             steps[name](*a)
-    xt_copy = local_copy(xt, xt_out, 9)
-    hd_copy = local_copy(hd, hd_out, 10)
+    xt_copy = local_copy(xt, xt_out, 2)
+    hd_copy = local_copy(hd, hd_out, 3)
+    ag_copies = []
     for t in range(2):
         with jax.named_scope("gathered%d" % t):
             gathered(2, t)
+            ag_copies.append(local_copy(ag.at[1, :, t], ag_out.at[:, t], t))
     with jax.named_scope("tail"):
-        ag_copy = local_copy(ag.at[1], ag_out, 11)
         left(xs.at[:, pl.ds(0, 120), :], xsem.at[0])
         left(sbuf, rss)
         left(pbuf, pss)
@@ -441,7 +450,8 @@
         left(gs.at[:, :, pl.ds(0, 120), :], gss)
         xt_copy.wait()
         hd_copy.wait()
-        ag_copy.wait()
+        for c in ag_copies:
+            c.wait()
 
 
 def weights_kernel(xt, ag, hd, gate_out, up_out, down_out, buf, sem):
@@ -503,14 +513,14 @@
             pltpu.VMEM((2, 2, 8, 8, DL), BF16),
             pltpu.VMEM((2, 2, 8, 8, DL), BF16),
             pltpu.VMEM((2, 2, 128, DL), BF16),
-            dma((12,)),
-            dma((4,)),
+            dma((9,)),
+            dma((2,)),
             dma, dma,
             dma((2, 2, 3)),
             dma((2,)),
-            dma, dma((2, 8)),
+            dma, dma((2, 3)),
             dma, dma((2, 2, 4)),
-            dma, dma((2, 2, 2, 2)), dma, dma((2, 2)),
+            dma, dma((2, 2, 3)), dma, dma((2, 2)),
             dma,
             dma((2, 3, 3)),
             dma((2,)), dma((2, 2, 2)),

time: 88.4 us -> 88.8 us (level)
  no operation moved by 1% of the time
where the time goes in v6:
time: 88.8 us; the launch traced here: 88.5 us
  Pallas kernels  87.9 us (99%)
    pallas_call x1, Pallas kernels, body(): pl.pallas_call(kernel, out_shape=(jax.ShapeDtypeStruct((DL, TOKENS), BF16...  86.3 us

profile of v6, /device:TPU:32, one launch (start us, length us, event | category | flops | bytes accessed | tf_op | source)
XLA Modules:
  0.0 88.5 jit_solution(14235410790818614774)
XLA Ops:
  0.6 86.3 %shard_map.103 = (bf16[512,256]{1,0:T(8,128)(2,1)S(1)}, bf16[2,2,128,896]{3,2,1,0:T(8,128)(2,1)S(1)}, bf16[896,512]{1,0:T(8,128)(2,1)S(1)}) custom-call(bf16[16,512]{1,0:T(8,128)(2,1)} %tok.1, bf16[16,512]{1,0:T(8,128)(2,1)} %tgt.1, bf16[512,896]{1,0:T(8,128)(2,1)} %wg.1, bf16[512,896]{1,0:T(8,128)(2,1)} %wu.1, bf16[896,512]{1,0:T(8,128)(2,1)} %wd.1, ...), custom_call_target="tpu_custom_call" | custom-call | tf_op jit(solution)/shard_map/pallas_call | solution.py:479
  86.9 1.6 %shard_map.104 = (bf16[512,896]{1,0:T(8,128)(2,1)}, bf16[512,896]{1,0:T(8,128)(2,1)}, bf16[896,512]{1,0:T(8,128)(2,1)}) custom-call(bf16[512,256]{1,0:T(8,128)(2,1)S(1)} %get-tuple-element.6.xt, bf16[2,256,896]{2,1,0:T(8,128)(2,1)S(1)} %bitcast.1, bf16[896,512]{1,0:T(8,128)(2,1)S(1)} %get-tuple-element.8.hd), custom_call_target="tpu_custom_call" | custom-call | tf_op jit(solution)/shard_map/pallas_call | solution.py:533

commit v7 on v6

--- a/solution.py
+++ b/solution.py
@@ -136,11 +136,14 @@
     all_far = (8, 10, 6, 9, 7, 11, 5, 12, 4, 14, 2, 13, 3, 15, 1)
 
     with jax.named_scope("tokens"):
-        for c in own_tok:
-            c.wait()
-        for k in all_far:
-            send(xs.at[:, own8, :], xs.at[:, own8, :], xsem.at[0], xsem.at[1], at_gy(lax.rem(h + k, NG)))
-        arrived(xs.at[:, pl.ds(0, 120), :], xsem.at[1])
+        for t in range(2):
+            own_tok[t].wait()
+            block = xs.at[t, own8, :]
+            for k in all_far:
+                send(block, block, xsem.at[0], xsem.at[1 + t], at_gy(lax.rem(h + k, NG)))
+
+    def tokens_in(t):
+        arrived(xs.at[t, pl.ds(0, 120), :], xsem.at[1 + t])
 
     slots = {}
 
@@ -390,6 +393,8 @@
         if t == 0:
             local[2 * q].wait()
             local[2 * q + 1].wait()
+        if q == 1:
+            tokens_in(t)
         up(t, q)
 
     def out_waited(t, w):
@@ -514,7 +519,7 @@
             pltpu.VMEM((2, 2, 8, 8, DL), BF16),
             pltpu.VMEM((2, 2, 128, DL), BF16),
             dma((9,)),
-            dma((2,)),
+            dma((3,)),
             dma, dma,
             dma((2, 2, 3)),
             dma((2,)),

time: 88.8 us -> 87.2 us (0.982)
  Pallas kernels: 87.9 us -> 86.4 us
    pallas_call x1, Pallas kernels: 86.3 us -> 84.8 us  [body(): pl.pallas_call(kernel, out_shape=(jax.ShapeDtypeStruct((DL, TOKENS), BF16...]
where the time goes in v7:
time: 87.2 us; the launch traced here: 87.1 us
  Pallas kernels  86.4 us (99%)
    pallas_call x1, Pallas kernels, body(): pl.pallas_call(kernel, out_shape=(jax.ShapeDtypeStruct((DL, TOKENS), BF16...  84.8 us

profile of v7, /device:TPU:32, one launch (start us, length us, event | category | flops | bytes accessed | tf_op | source)
XLA Modules:
  0.0 87.1 jit_solution(8506493382906862768)
XLA Ops:
  0.6 84.8 %shard_map.103 = (bf16[512,256]{1,0:T(8,128)(2,1)S(1)}, bf16[2,2,128,896]{3,2,1,0:T(8,128)(2,1)S(1)}, bf16[896,512]{1,0:T(8,128)(2,1)S(1)}) custom-call(bf16[16,512]{1,0:T(8,128)(2,1)} %tok.1, bf16[16,512]{1,0:T(8,128)(2,1)} %tgt.1, bf16[512,896]{1,0:T(8,128)(2,1)} %wg.1, bf16[512,896]{1,0:T(8,128)(2,1)} %wu.1, bf16[896,512]{1,0:T(8,128)(2,1)} %wd.1, ...), custom_call_target="tpu_custom_call" | custom-call | tf_op jit(solution)/shard_map/pallas_call | solution.py:484
  85.5 1.6 %shard_map.104 = (bf16[512,896]{1,0:T(8,128)(2,1)}, bf16[512,896]{1,0:T(8,128)(2,1)}, bf16[896,512]{1,0:T(8,128)(2,1)}) custom-call(bf16[512,256]{1,0:T(8,128)(2,1)S(1)} %get-tuple-element.6.xt, bf16[2,256,896]{2,1,0:T(8,128)(2,1)S(1)} %bitcast.1, bf16[896,512]{1,0:T(8,128)(2,1)S(1)} %get-tuple-element.8.hd), custom_call_target="tpu_custom_call" | custom-call | tf_op jit(solution)/shard_map/pallas_call | solution.py:538
